TPU v7x, 32 devices: a whole 2x2x4 slice. The times are simulated.
32 devices in a mesh: pairs: 16 (over z, y, x), comp: 2 (over core).
Axes of the slice: x: 2, y: 2, z: 4, core: 2. Of those that a mesh axis runs over, the one named last changes fastest.
Arguments:
- effects: float32 [49, 131072], P(None, 'pairs'), may hold values from -24 to 24
- se_table: float32 [16, 49], replicated, may hold values from 0.5 to 2
- se_index: int32 [256], P('pairs'), may hold values from 0 to 15
- base_root: float32 [16, 49, 49], replicated, may hold values from -0.875 to 0.875
- grid_scale: float32 [16], replicated, may hold values from 0.25 to 4
- comp_base: int32 [256], P('comp'), may hold values from 0 to 15
- comp_grid: int32 [256], P('comp'), may hold values from 0 to 15
- weights: float32 [256], P('comp'), may hold values from 0.2 to 5
Outputs:
- responsibility: float32 [256, 131072], P('comp', 'pairs')
- log_weights: float32 [256], P('comp')
- pair_loglik: float32 [131072], P('pairs')
All inputs are finite; a program needn't handle non-finite values.
Results may differ from a plain program's by a relative error of at most 0.0003.
Values sent between devices are 32-bit elements; how exact they have to be, the bound alone decides.
No kernel may reach another device: no remote copies, remote signals or barrier semaphores. Data moves between devices by JAX's collectives and lax.ppermute only.
A program may use at most 384 MiB of HBM per device.

v0:
```python
import math

import jax
import jax.numpy as jnp
from jax import lax
from jax.sharding import PartitionSpec as P

TILE = 512


def joined(part, axis, combine):
    gathered = jax.tree.map(lambda a: lax.all_gather(a, axis), part)

    def take(source):
        return jax.tree.map(lambda a: lax.dynamic_index_in_dim(a, source, 0, False), gathered)

    return lax.fori_loop(
        1, lax.axis_size(axis), lambda source, state: combine(state, take(source)), take(0)
    )


def build_factors(se_rows, covar_rows, scale_rows):
    tissues = se_rows.shape[1]
    identity = jnp.eye(tissues, dtype=jnp.float32)
    system = (scale_rows * scale_rows)[:, None, None] * covar_rows.reshape(-1, tissues, tissues)
    system = system + identity[None] * (se_rows * se_rows)[:, :, None]
    factor = jnp.linalg.cholesky(system)
    eye_full = jnp.broadcast_to(identity, factor.shape)
    inverse = jax.scipy.linalg.solve_triangular(factor, eye_full, lower=True)
    logdet = jnp.sum(jnp.log(jnp.diagonal(factor, axis1=1, axis2=2)), axis=1)
    return (inverse, logdet)


def exact_dot(left, right):
    return jnp.dot(left, right, precision=lax.Precision.HIGHEST, preferred_element_type=jnp.float32)


def per_device(effects, se_table, se_index, base_root, grid_scale, comp_base, comp_grid, weights):
    tissues = effects.shape[0]
    local_pairs = effects.shape[1]
    comp_count = comp_base.shape[0]
    block_count = se_table.shape[0]
    covariances = jnp.einsum("uij,ukj->uik", base_root, base_root, precision=lax.Precision.HIGHEST)
    covariances = covariances.reshape(covariances.shape[0], tissues * tissues)
    base_pick = (
        comp_base[:, None] == jnp.arange(covariances.shape[0], dtype=jnp.int32)[None]
    ).astype(jnp.float32)
    comp_covar = exact_dot(base_pick, covariances)
    grid_pick = (
        comp_grid[:, None] == jnp.arange(grid_scale.shape[0], dtype=jnp.int32)[None]
    ).astype(jnp.float32)
    comp_scale = exact_dot(grid_pick, grid_scale)
    item_share = block_count * comp_count // lax.axis_size("pairs")
    item_first = lax.axis_index("pairs") * item_share
    item_ids = item_first + jnp.arange(item_share, dtype=jnp.int32)
    block_pick = (
        (item_ids // comp_count)[:, None] == jnp.arange(block_count, dtype=jnp.int32)[None]
    ).astype(jnp.float32)
    item_pick = (
        (item_ids % comp_count)[:, None] == jnp.arange(comp_count, dtype=jnp.int32)[None]
    ).astype(jnp.float32)
    own_inverse, own_logdet = build_factors(
        exact_dot(block_pick, se_table),
        exact_dot(item_pick, comp_covar),
        exact_dot(item_pick, comp_scale),
    )
    inverse, logdet = (
        lax.all_gather(own_inverse, "pairs", axis=0, tiled=True),
        lax.all_gather(own_logdet, "pairs", axis=0, tiled=True),
    )
    whiten_table = inverse.reshape(block_count, comp_count, tissues, tissues).transpose(0, 3, 2, 1)
    whiten_table = whiten_table.reshape(block_count, tissues, tissues * comp_count)
    logdet_table = logdet.reshape(block_count, comp_count)
    log_prior = jnp.log(weights)
    constant = 0.5 * tissues * math.log(2.0 * math.pi)

    def one_tile(tile_id, scores):
        block_id = se_index[tile_id]
        block_table = lax.dynamic_index_in_dim(whiten_table, block_id, 0, keepdims=False)
        tile_data = lax.dynamic_slice_in_dim(effects, tile_id * TILE, TILE, 1)
        whitened = lax.dot_general(
            block_table,
            tile_data,
            (((0,), (0,)), ((), ())),
            precision=lax.Precision.HIGHEST,
            preferred_element_type=jnp.float32,
        )
        whitened = whitened.reshape(tissues, comp_count, TILE)
        quadratic = jnp.sum(whitened * whitened, axis=0)
        logdet_row = lax.dynamic_index_in_dim(logdet_table, block_id, 0, keepdims=False)
        tile_scores = log_prior[:, None] - 0.5 * quadratic - logdet_row[:, None] - constant
        return lax.dynamic_update_slice_in_dim(scores, tile_scores, tile_id * TILE, 1)

    scores = lax.fori_loop(
        0, local_pairs // TILE, one_tile, jnp.zeros((comp_count, local_pairs), jnp.float32)
    )
    local_max = jnp.max(scores, axis=0)
    local_sum = jnp.sum(jnp.exp(scores - local_max), axis=0)

    def combine(former, latter):
        larger = jnp.maximum(former[0], latter[0])
        return (
            larger,
            former[1] * jnp.exp(former[0] - larger) + latter[1] * jnp.exp(latter[0] - larger),
        )

    score_max, score_sum = joined((local_max, local_sum), "comp", combine)
    pair_loglik = score_max + jnp.log(score_sum)
    responsibility = jnp.exp(scores - pair_loglik)
    masses = lax.psum(jnp.sum(responsibility, axis=1), "pairs")
    all_pairs = local_pairs * lax.axis_size("pairs")
    all_comps = comp_count * lax.axis_size("comp")
    log_weights = jnp.log((masses + 1.0) / (all_pairs + all_comps))
    return (responsibility, log_weights, pair_loglik)


def solution(mesh):
    placed = (P(None, "pairs"), P(), P("pairs"), P(), P(), P("comp"), P("comp"), P("comp"))
    return jax.shard_map(
        per_device,
        mesh=mesh,
        in_specs=placed,
        out_specs=(P("comp", "pairs"), P("comp"), P("pairs")),
        check_vma=False,
    )
```

profile of v0, /device:TPU:0, one launch (start us, length us, event | category | flops | bytes accessed | tf_op | source)
XLA Modules:
  0.0 1578.0 jit_solution(9261916296940407890)
XLA Ops:
  35.2 576.8 %custom-call.8 = f32[128,49,49]{2,1,0:T(8,128)} custom-call(f32[128,49,49]{2,1,0:T(8,128)} %fusion.5), custom_call_target="Cholesky" | custom-call | tf_op jit(solution)/shard_map/jit(cholesky)/cholesky | solution.py:27
  618.5 37.6 %custom-call.9 = f32[128,1,49,49]{0,2,3,1:T(8,128)S(1)} custom-call(f32[128,1,49,49]{0,3,2,1:T(8,128)} %get-tuple-element.235), custom_call_target="InvertDiagBlocksLowerTriangular" | custom-call | tf_op jit(solution)/shard_map/jit(_solve_triangular)/vmap()/triangular_solve | solution.py:29
  675.0 59.4 %all-gather.2 = f32[16,1,128]{2,1,0:T(1,128)S(1)} all-gather(f32[1,1,128]{2,1,0:T(1,128)S(1)} %bitcast.70), channel_id=1, replica_groups=mesh['pairs'=16,'comp'=2] {'pairs'}, dimensions={0}, use_global_device_ids=true | all-gather | bytes 8704 | tf_op jit(solution)/shard_map/all_gather | solution.py:69
  734.4 403.9 %all-gather.5.cloned.1.call-done = f32[2048,49,49]{0,2,1:T(8,128)} async-done(((f32[128,49,49]{0,2,1:T(8,128)}), f32[2048,49,49]{0,2,1:T(8,128)}) %all-gather.5.cloned.1.call-update) | async-done | bytes 19669008 | tf_op jit(solution)/shard_map/all_gather | solution.py:68
  1138.3 21.0 %reshape.91 = f32[16,128,49,49]{1,0,3,2:T(8,128)} reshape(f32[2048,49,49]{0,2,1:T(8,128)} %all-gather.5.cloned.1.call-done) | data formatting | bytes 39337984 | tf_op jit(solution)/shard_map/reshape | solution.py:71
  1159.2 21.0 %copy.72 = f32[16,128,49,49]{1,2,0,3:T(8,128)} copy(f32[16,128,49,49]{1,0,3,2:T(8,128)} %reshape.91) | data formatting | bytes 39337984 | tf_op jit(solution)/shard_map/reshape | solution.py:71
  1180.2 22.4 %reshape.92 = f32[16,49,6272]{2,0,1:T(8,128)} reshape(f32[16,49,49,128]{3,2,0,1:T(8,128)} %bitcast.62) | data formatting | bytes 39337984 | tf_op jit(solution)/shard_map/reshape | solution.py:72
  1205.1 313.8 %while.10 = (s32[]{:T(128)}, f32[128,8192]{1,0:T(8,128)}, f32[128]{0:T(128)S(1)}, s32[16]{0:T(128)S(1)}, f32[16,49,6272]{2,0,1:T(8,128)}, /*index=5*/f32[49,8192...) while((s32[]{:T(128)}, f32[128,8192]{1,0:T(8,128)}, ...), condition=%wide.region_5.6_spmd, body=%wide.region_3.5_spmd.sunk | while | flops 1894842368 | bytes 9508585 | solution.py:94
  1232.2 11.3 multiply_reduce_fusion.2
  1251.8 11.3 multiply_reduce_fusion.2
  1271.4 11.3 multiply_reduce_fusion.2
  1291.0 11.3 multiply_reduce_fusion.2
  1310.6 11.3 multiply_reduce_fusion.2
  1330.3 11.3 multiply_reduce_fusion.2
  1349.9 11.3 multiply_reduce_fusion.2
  1369.5 11.3 multiply_reduce_fusion.2
  1389.1 11.3 multiply_reduce_fusion.2
  1408.7 11.3 multiply_reduce_fusion.2
  1428.3 11.3 multiply_reduce_fusion.2
  1447.9 11.3 multiply_reduce_fusion.2
  1467.5 11.3 multiply_reduce_fusion.2
  1487.2 11.3 multiply_reduce_fusion.2
  1506.8 11.3 multiply_reduce_fusion.2
  1531.3 39.3 %psum.7 = f32[128]{0:T(128)S(1)} all-reduce(f32[128]{0:T(128)S(1)} %get-tuple-element.233), channel_id=1, replica_groups=mesh['pairs'=16,'comp'=2] {'pairs'}, use_global_device_ids=true, to_apply=%region_9.10 | all-reduce | flops 128 | bytes 1024 | tf_op jit(solution)/shard_map/psum | solution.py:110
  (147 shorter events, 181.6 us)
Async XLA Ops:
  7.2 0.7 copy-start
  7.2 1131.1 %all-gather.5.cloned.1.call-start = ((), (), s32[]{:S(2)}) async-start(), calls=%async_computation | async-start | bytes 23883776 | tf_op jit(solution)/shard_map/all_gather | solution.py:68
  669.3 4.6 copy-start.3
  1202.6 2.5 copy-start.4
  1521.3 7.5 copy-start.2
  1528.8 42.4 %copy-start.1 = (f32[16,49]{1,0:T(8,128)S(1)}, f32[16,49]{1,0:T(8,128)}, u32[]{:S(2)}) copy-start(f32[16,49]{1,0:T(8,128)} %param.11) | copy-start | bytes 9412
Sparse Core Ops, SparseCore 0:
  674.0 464.2 all-gather.4
where the time goes:
time: 1580 us
  other arithmetic  649 us (41%)
  waiting for transfers between devices  404 us (26%)
  matrix products  196 us (12%)
  local copies, waits for them, and re-layouts  181 us (11%)
  blocking collectives  102 us (6%)
  loops' own time  31.6 us (2%)
    another operation x4, other arithmetic, build_factors(): factor = jnp.linalg.cholesky(system)  577 us
    all_gather x1, waiting for transfers between devices, per_device(): lax.all_gather(own_inverse, 'pairs', axis=0, tiled=True)  404 us
    dot_general x16, matrix products, one_tile(): lax.dot_general(block_table, tile_data, (((0,), (0,)), ((), ())), precisi...  181 us
    dynamic_slice x32, local copies, waits for them, and re-layouts, one_tile(): lax.dynamic_index_in_dim(whiten_table, block_id, 0, keepdims=False)  76 us
    all_gather x1, blocking collectives, per_device(): lax.all_gather(own_logdet, 'pairs', axis=0, tiled=True)  59.4 us
    reshape x2, local copies, waits for them, and re-layouts, per_device(): inverse.reshape(block_count, comp_count, tissues, tissues)  42 us
    psum x1, blocking collectives, per_device(): masses = lax.psum(jnp.sum(responsibility, axis=1), 'pairs')  39.3 us
    another operation x3, other arithmetic, build_factors(): inverse = jax.scipy.linalg.solve_triangular(factor, eye_full, lower=True)  39.1 us
  transfers between devices with their start and end apart: 1, of which 1 were waited for; matrix products, arithmetic and copies ran while one was open for 0% of the time, Pallas kernels for 0%

commit v1 on v0

v1 whole, which is shorter than its diff:
```python
import functools
import math

import jax
import jax.numpy as jnp
from jax import lax
from jax.experimental import pallas as pl
from jax.experimental.pallas import tpu as pltpu
from jax.sharding import PartitionSpec as P

TILE = 512
SUB = 8
LANES = 128
PIECES = 5


def block_edge(count):
    return max(edge for edge in range(1, 9) if count % edge == 0)


def element(index):
    return pl.ds(pl.multiple_of(index * SUB, SUB), SUB)


def eliminate(n, table, pivots, factors):
    edge = block_edge(n)
    blocks = n // edge

    def at(i, j):
        return element(i * n + j)

    def one_pivot_block(kb, carry):
        first = kb * edge
        diag = [[table[at(first + m, first + j), :] if j >= m else None for j in range(edge)] for m in range(edge)]
        lower = [[None] * edge for _ in range(edge)]
        inverse = [[None] * edge for _ in range(edge)]
        recips = []
        for m in range(edge):
            d = diag[m][m]
            recip = 1.0 / d
            recips.append(recip)
            pivots[element(first + m), :] = d
            for r in range(m + 1, edge):
                lower[r][m] = diag[m][r] * recip
            for r in range(m + 1, edge):
                for j in range(r, edge):
                    diag[r][j] = diag[r][j] - lower[r][m] * diag[m][j]
                for j in range(m):
                    inverse[r][j] = inverse[r][j] - lower[r][m] * inverse[m][j]
                inverse[r][m] = -lower[r][m]
        for r in range(edge):
            for j in range(r):
                table[at(first + r, first + j), :] = inverse[r][j]

        def column_block(jb, with_factor):
            col = jb * edge
            for j in range(edge):
                rows = [table[at(first + m, col + j), :] for m in range(edge)]
                for m in range(edge):
                    for r in range(m + 1, edge):
                        rows[r] = rows[r] - lower[r][m] * rows[m]
                for m in range(edge):
                    if m:
                        table[at(first + m, col + j), :] = rows[m]
                    if with_factor:
                        factors[element(m * n + col + j), :] = rows[m] * recips[m]

        def left(jb, c):
            column_block(jb, False)
            return c

        def right(jb, c):
            column_block(jb, True)
            return c

        lax.fori_loop(0, kb, left, 0)
        lax.fori_loop(kb + 1, blocks, right, 0)

        def row_block(ib, c):
            row = ib * edge
            for i in range(edge):
                f = [factors[element(m * n + row + i), :] for m in range(edge)]
                for j in range(edge):
                    total = f[j]
                    for m in range(j + 1, edge):
                        total = total + f[m] * inverse[m][j]
                    table[at(row + i, first + j), :] = -total

            for i in range(edge):
                f = [factors[element(m * n + row + i), :] for m in range(edge)]
                for j in range(i, edge):
                    value = table[at(row + i, row + j), :]
                    for m in range(edge):
                        value = value - f[m] * table[at(first + m, row + j), :]
                    table[at(row + i, row + j), :] = value

            def full(index, cc):
                jb = jnp.where(index < kb, index, index - kb + ib + 1)
                col = jb * edge
                start = 0
                for size in (edge - edge // 2, edge // 2):
                    rows = range(start, start + size)
                    start += size
                    held = [[table[at(row + i, col + j), :] for j in range(edge)] for i in rows]
                    for m in range(edge):
                        f = [factors[element(m * n + row + i), :] for i in rows]
                        for j in range(edge):
                            u = table[at(first + m, col + j), :]
                            for a in range(len(f)):
                                held[a][j] = held[a][j] - f[a] * u
                    for a, i in enumerate(rows):
                        for j in range(edge):
                            table[at(row + i, col + j), :] = held[a][j]
                return cc

            lax.fori_loop(0, kb + blocks - 1 - ib, full, 0)
            return c

        lax.fori_loop(kb + 1, blocks, row_block, 0)
        return carry

    lax.fori_loop(0, blocks, one_pivot_block, 0)


def split3(value):
    one = value.astype(jnp.bfloat16)
    rest = value - one.astype(jnp.float32)
    two = rest.astype(jnp.bfloat16)
    three = (rest - two.astype(jnp.float32)).astype(jnp.bfloat16)
    return one, two, three


def main_kernel(
    n, tiles, patterns,
    index_ref, effects_ref, se_ref, covar_ref, prior_ref,
    out_ref, max_ref, sum_ref,
    table, pivots, factors, roots, halfdet, noise, weights, flipped, stack, acc, se_rows,
    count_s, start_s, slot_s, order_s,
):
    comps = LANES
    even = n // 16 * 16
    edge_rows = n - even

    def clear(b, c):
        count_s[b] = 0
        return c

    lax.fori_loop(0, patterns, clear, 0)

    def tally(t, c):
        b = index_ref[t]
        count_s[b] = count_s[b] + 1
        return c

    lax.fori_loop(0, tiles, tally, 0)

    def place(b, state):
        used, offset = state
        many = count_s[b]
        slot_s[used] = b
        start_s[used] = offset
        count_s[b] = offset
        return used + jnp.where(many > 0, 1, 0), offset + many

    used, _ = lax.fori_loop(0, patterns, place, (jnp.int32(0), jnp.int32(0)))
    start_s[used] = tiles

    def sort(t, c):
        b = index_ref[t]
        position = count_s[b]
        order_s[position] = t
        count_s[b] = position + 1
        return c

    lax.fori_loop(0, tiles, sort, 0)

    weights[...] = jnp.zeros_like(weights)
    stack[...] = jnp.zeros_like(stack)

    def one_batch(batch, carry):
        base = batch * SUB
        for s in range(SUB):
            b = slot_s[jnp.minimum(base + s, used - 1)]
            se_rows[pl.ds(s, 1), :] = se_ref[pl.ds(b, 1), :]
        ses = se_rows[...]
        squares = ses * ses
        for i in range(n):
            noise[pl.ds(i * SUB, SUB), :] = jnp.broadcast_to(squares[:, i : i + 1], (SUB, LANES))

        def fill_row(i, c):
            def fill(j, cc):
                e = i * n + j
                table[element(e), :] = covar_ref[pl.ds(e, SUB, stride=0), :]
                return cc

            def fill_block(jb, cc):
                for a in range(block_edge(n)):
                    fill(jb * block_edge(n) + a, 0)
                return cc

            lax.fori_loop(i // block_edge(n), n // block_edge(n), fill_block, 0)
            d = element(i * n + i)
            table[d, :] = table[d, :] + noise[element(i), :]
            return c

        lax.fori_loop(0, n, fill_row, 0)
        eliminate(n, table, pivots, factors)
        logs = jnp.zeros((SUB, LANES), jnp.float32)
        for i in range(n):
            d = pivots[pl.ds(i * SUB, SUB), :]
            roots[pl.ds(i * SUB, SUB), :] = lax.rsqrt(d)
            logs = logs + jnp.log(d)
        halfdet[...] = prior_ref[...] - 0.5 * logs

        def one_slot(slot, c):
            s = slot - base
            for i in range(n):
                groups = min(i // 16 + 1, even // 16)
                rows = groups * 16
                root = roots[pl.ds(i * SUB + s, SUB, stride=0), :][0:1, :]
                row = table[pl.ds(i * n * SUB + s, rows, stride=SUB), :]
                if i < even:
                    j = lax.broadcasted_iota(jnp.int32, (rows, LANES), 0)
                    row = jnp.where(j < i, row, jnp.where(j == i, 1.0, 0.0))
                row = row * root
                one = row.astype(jnp.bfloat16)
                two = (row - one.astype(jnp.float32)).astype(jnp.bfloat16)
                for piece, part in enumerate((one, one, two, two, one)):
                    weights[i, pl.ds(piece * even, rows), :] = part
                if i >= even:
                    first = root.astype(jnp.bfloat16)
                    second = (root - first.astype(jnp.float32)).astype(jnp.bfloat16)
                    j = lax.broadcasted_iota(jnp.int32, (16, LANES), 0)
                    tail = jnp.zeros((16, LANES), jnp.float32)
                    for piece, part in enumerate((first, first, second, second, first)):
                        tail = jnp.where(j == piece, part.astype(jnp.float32), tail)
                    weights[i, pl.ds(PIECES * even, 16), :] = tail.astype(jnp.bfloat16)
            row_const = halfdet[pl.ds(s, 1), :]

            def one_tile(place_at, cc):
                t = order_s[place_at]
                at = pl.ds(pl.multiple_of(t * TILE, TILE), TILE)
                data = effects_ref[pl.ds(0, even), at]
                x1, x2, x3 = split3(data)
                for piece, part in enumerate((x1, x2, x1, x2, x3)):
                    stack[pl.ds(piece * even, even), :] = part.astype(jnp.float32)
                for extra in range(edge_rows):
                    line = effects_ref[pl.ds(even + extra, 1), at]
                    x1, x2, x3 = split3(line)
                    for piece, part in enumerate((x1, x2, x1, x2, x3)):
                        stack[pl.ds(PIECES * even + extra * PIECES + piece, 1), :] = part.astype(jnp.float32)
                flipped[...] = jnp.transpose(stack[...]).astype(jnp.bfloat16)
                for i in range(0, n, 2):
                    if i + 1 < n:
                        right = jnp.concatenate([weights[i], weights[i + 1]], axis=1)
                    else:
                        right = weights[i]
                    white = jnp.dot(flipped[...], right, preferred_element_type=jnp.float32)
                    square = white[:, :LANES] * white[:, :LANES]
                    if i + 1 < n:
                        square = square + white[:, LANES:] * white[:, LANES:]
                    if i:
                        acc[...] += square
                    else:
                        acc[...] = square
                scores = jnp.transpose(row_const - 0.5 * acc[...])
                top = jnp.max(scores, axis=0, keepdims=True)
                shifted = jnp.exp(scores - top)
                out_ref[:, at] = shifted
                max_ref[:, at] = top
                sum_ref[:, at] = jnp.sum(shifted, axis=0, keepdims=True)
                return cc

            lax.fori_loop(start_s[slot], start_s[slot + 1], one_tile, 0)
            return c

        lax.fori_loop(base, jnp.minimum(used, base + SUB), one_slot, 0)
        return carry

    lax.fori_loop(0, (used + SUB - 1) // SUB, one_batch, 0)


def shifted_scores(effects, se_table, se_index, covar, prior):
    n, pairs = effects.shape
    patterns = se_table.shape[0]
    tiles = pairs // TILE
    even = n // 16 * 16
    assert covar.shape == (n * n, LANES) and (n - even) * PIECES <= 16
    depth = PIECES * even + 16
    se_wide = jnp.pad(se_table, ((0, 0), (0, LANES - n)))
    vmem = pl.BlockSpec(memory_space=pltpu.VMEM)
    smem = pl.BlockSpec(memory_space=pltpu.SMEM)
    f32 = jnp.float32
    return pl.pallas_call(
        functools.partial(main_kernel, n, tiles, patterns),
        name="shifted_scores",
        out_shape=(
            jax.ShapeDtypeStruct((LANES, pairs), f32),
            jax.ShapeDtypeStruct((1, pairs), f32),
            jax.ShapeDtypeStruct((1, pairs), f32),
        ),
        in_specs=[smem, vmem, vmem, vmem, vmem],
        out_specs=(vmem, vmem, vmem),
        scratch_shapes=[
            pltpu.VMEM((n * n * SUB, LANES), f32),
            pltpu.VMEM((n * SUB, LANES), f32),
            pltpu.VMEM((block_edge(n) * n * SUB, LANES), f32),
            pltpu.VMEM((n * SUB, LANES), f32),
            pltpu.VMEM((SUB, LANES), f32),
            pltpu.VMEM((n * SUB, LANES), f32),
            pltpu.VMEM((n, depth, LANES), jnp.bfloat16),
            pltpu.VMEM((TILE, depth), jnp.bfloat16),
            pltpu.VMEM((depth, TILE), f32),
            pltpu.VMEM((TILE, LANES), f32),
            pltpu.VMEM((SUB, LANES), f32),
            pltpu.SMEM((patterns + 1,), jnp.int32),
            pltpu.SMEM((patterns + 1,), jnp.int32),
            pltpu.SMEM((patterns + 1,), jnp.int32),
            pltpu.SMEM((tiles,), jnp.int32),
        ],
        compiler_params=pltpu.CompilerParams(vmem_limit_bytes=60 * 1024 * 1024),
    )(se_index, effects, se_wide, covar, prior)


def exact_dot(left, right, dims):
    return lax.dot_general(left, right, (dims, ((), ())), precision=lax.Precision.HIGHEST, preferred_element_type=jnp.float32)


def finish_kernel(shifted_ref, scale_ref, out_ref, mass_ref):
    value = shifted_ref[...] * scale_ref[...]
    out_ref[...] = value
    total = jnp.sum(value, axis=1, keepdims=True)

    @pl.when(pl.program_id(0) == 0)
    def _():
        mass_ref[...] = jnp.zeros_like(mass_ref)

    mass_ref[...] += total


def finish(shifted, scale):
    comps, pairs = shifted.shape
    width = min(pairs, 1024)
    return pl.pallas_call(
        finish_kernel,
        name="finish",
        grid=(pairs // width,),
        in_specs=[
            pl.BlockSpec((comps, width), lambda g: (0, g)),
            pl.BlockSpec((1, width), lambda g: (0, g)),
        ],
        out_specs=(
            pl.BlockSpec((comps, width), lambda g: (0, g)),
            pl.BlockSpec((comps, 1), lambda g: (0, 0)),
        ),
        out_shape=(
            jax.ShapeDtypeStruct((comps, pairs), jnp.float32),
            jax.ShapeDtypeStruct((comps, 1), jnp.float32),
        ),
    )(shifted, scale)


def per_device(effects, se_table, se_index, base_root, grid_scale, comp_base, comp_grid, weights):
    n, pairs = effects.shape
    comps = comp_base.shape[0]
    covariances = jnp.einsum("uij,ukj->uik", base_root, base_root, precision=lax.Precision.HIGHEST)
    covariances = covariances.reshape(covariances.shape[0], n * n)
    bases = jnp.arange(covariances.shape[0], dtype=jnp.int32)
    grids = jnp.arange(grid_scale.shape[0], dtype=jnp.int32)
    scale = jnp.sum(jnp.where(comp_grid[None] == grids[:, None], grid_scale[:, None], 0.0), axis=0)
    pick = (comp_base[None] == bases[:, None]).astype(jnp.float32)
    covar = exact_dot(covariances, pick, ((0,), (0,))) * (scale * scale)[None]
    prior = (jnp.log(weights) - 0.5 * n * math.log(2.0 * math.pi))[None]
    shifted, top, total = shifted_scores(effects, se_table, se_index, covar, prior)
    both = lax.all_gather(jnp.concatenate([top, total], axis=0), "comp")
    tops, totals = both[:, 0], both[:, 1]
    score_max = jnp.max(tops, axis=0)
    score_sum = jnp.sum(totals * jnp.exp(tops - score_max), axis=0)
    pair_loglik = score_max + jnp.log(score_sum)
    responsibility, mass = finish(shifted, jnp.exp(top - pair_loglik[None]))
    masses = lax.psum(mass[:, 0], "pairs")
    all_pairs = pairs * lax.axis_size("pairs")
    all_comps = comps * lax.axis_size("comp")
    log_weights = jnp.log((masses + 1.0) / (all_pairs + all_comps))
    return (responsibility, log_weights, pair_loglik)


def solution(mesh):
    placed = (P(None, "pairs"), P(), P("pairs"), P(), P(), P("comp"), P("comp"), P("comp"))
    return jax.shard_map(
        per_device,
        mesh=mesh,
        in_specs=placed,
        out_specs=(P("comp", "pairs"), P("comp"), P("pairs")),
        check_vma=False,
    )
```

time: 1580 us -> 145 us (0.09)
  other arithmetic: 649 us -> 6 us
  waiting for transfers between devices: 404 us -> 0 us
  matrix products: 196 us -> 4.39 us
  local copies, waits for them, and re-layouts: 181 us -> 1.47 us
  Pallas kernels: 0 us -> 86 us
  blocking collectives: 102 us -> 45.6 us
  loops' own time: 31.6 us -> 0 us
    another operation x7 -> x0, other arithmetic: 617 us -> none  [the longest x4 577 us: build_factors(): factor = jnp.linalg.cholesky(system)]
    all_gather x1 -> x0, waiting for transfers between devices: 404 us -> none  [per_device(): lax.all_gather(own_inverse, 'pairs', axis=0, tiled=True)]
    dot_general x21 -> x1, matrix products: 185 us -> 2.2 us  [exact_dot(): lax.dot_general(left, right, (dims, ((), ())), precision=lax.Precision.HI...]
    pallas_call x0 -> x2, Pallas kernels: none -> 86 us  [the longest x1 79.1 us: shifted_scores(): pl.pallas_call(functools.partial(main_kernel, n, tiles, patterns), name='...]
    dynamic_slice x48 -> x0, local copies, waits for them, and re-layouts: 85.3 us -> none  [the longest x32 76 us: one_tile(): lax.dynamic_index_in_dim(whiten_table, block_id, 0, keepdims=False)]
    reshape x6 -> x1, local copies, waits for them, and re-layouts: 69.2 us -> 0.17 us  [per_device(): covariances = covariances.reshape(covariances.shape[0], n * n)]
    all_gather x3 -> x1, blocking collectives: 63.1 us -> 2.04 us  [per_device(): both = lax.all_gather(jnp.concatenate([top, total], axis=0), 'comp')]
    another operation x1 -> x0, loops' own time: 31.6 us -> none  [per_device(): lax.fori_loop(0, local_pairs // TILE, one_tile, jnp.zeros((comp_count, lo...]
  transfers between devices with their start and end apart: 1 -> 0, of which waited for: 1 -> 0; matrix products, arithmetic and copies ran while one was open for 0% -> 0% of each run, Pallas kernels for 0% -> 0%
where the time goes in v1:
time: 145 us; the launch traced here: 144 us
  Pallas kernels  86 us (59%)
  blocking collectives  45.6 us (31%)
  other arithmetic  6 us (4%)
  matrix products  4.39 us (3%)
  local copies, waits for them, and re-layouts  1.47 us (1%)
    pallas_call x1, Pallas kernels, shifted_scores(): pl.pallas_call(functools.partial(main_kernel, n, tiles, patterns), name='...  79.1 us
    psum x1, blocking collectives, per_device(): masses = lax.psum(mass[:, 0], 'pairs')  43.6 us
    pallas_call x1, Pallas kernels, finish(): pl.pallas_call(finish_kernel, name='finish', grid=(pairs // width,), in_s...  6.91 us

profile of v1, /device:TPU:0, one launch (start us, length us, event | category | flops | bytes accessed | tf_op | source)
XLA Modules:
  0.0 144.2 jit_solution(18319416780601691165)
XLA Ops:
  0.6 0.0 copy-start.1
  0.6 0.8 select_reduce_fusion
  1.4 1.2 add_bitcast_fusion.prior_ref
  2.6 1.3 pad.4.se_ref
  3.9 2.2 %fusion = f32[16,49,49]{2,1,0:T(8,128)S(1)} fusion(f32[16,49,49]{2,0,1:T(8,128)} %param.11), kind=kOutput, calls=%fused_computation.1 | convolution fusion | flops 22588608 | bytes 307328 | tf_op jit(solution)/shard_map/uij,ukj->uik/dot_general | solution.py:366
  6.1 0.2 reshape.32
  6.2 0.0 copy-done.1
  6.3 2.2 %convolution_multiply_fusion.covar_ref = f32[2401,128]{1,0:T(8,128)} fusion(f32[16,2401]{1,0:T(8,128)S(1)} %reshape.32, f32[128]{0:T(128)S(1)} %mul.18, s32[128]{0:T(128)S(1)} %copy-done.1), kind=kOutput, calls=%fused_computation | convolution fusion | flops 59316352 | bytes 1384000 | tf_op jit(solution)/shard_map/dot_general | solution.py:326
  8.5 79.1 %shifted_scores.1 = (f32[128,8192]{1,0:T(8,128)}, f32[1,8192]{1,0:T(1,128)}, f32[1,8192]{1,0:T(1,128)}) custom-call(s32[16]{0:T(128)} %index_ref.1, f32[49,8192]{1,0:T(8,128)} %effects_ref.1, f32[16,128]{1,0:T(8,128)} %pad.4.se_ref, f32[2401,128]{1,0:T(8,128)} %convolution_multiply_fusion.covar_ref, f32[1,128]{1,0:T(1,128)} %add_bitcast_fusion.prior_ref), custom_call_target="tpu_custom_call" | custom-call | tf_op jit(solution)/shard_map/shifted_scores/pallas_call | solution.py:294
  87.5 0.8 maximum_bitcast_fusion
  88.4 2.0 %all-gather.1 = f32[2,2,8192]{2,1,0:T(2,128)S(1)} all-gather(f32[1,2,8192]{2,1,0:T(2,128)S(1)} %maximum_bitcast_fusion), channel_id=2, replica_groups=mesh['pairs'=16,'comp'=2] {'comp'}, dimensions={0}, use_global_device_ids=true | all-gather | bytes 196608 | tf_op jit(solution)/shard_map/all_gather | solution.py:375
  90.4 0.2 fusion.6
  90.6 0.2 fusion.3
  90.8 0.0 copy-start
  90.8 1.4 subtract_exponential_fusion.scale_ref
  92.2 6.9 %finish.1 = (f32[128,8192]{1,0:T(8,128)}, f32[128,1]{1,0:T(8,128)}) custom-call(f32[128,8192]{1,0:T(8,128)} %get-tuple-element.8.shifted_ref, f32[1,8192]{1,0:T(1,128)} %subtract_exponential_fusion.scale_ref), custom_call_target="tpu_custom_call" | custom-call | tf_op jit(solution)/shard_map/finish/pallas_call | solution.py:344
  99.1 0.0 copy-done
  99.1 0.9 reduce.1
  100.1 43.6 %psum.7 = f32[128]{0:T(128)S(1)} all-reduce(f32[128]{0:T(128)S(1)} %reduce.1), channel_id=1, replica_groups=mesh['pairs'=16,'comp'=2] {'pairs'}, use_global_device_ids=true, to_apply=%region_3.4 | all-reduce | flops 128 | bytes 1024 | tf_op jit(solution)/shard_map/psum | solution.py:381
  143.6 0.5 multiply_log_fusion
  (2 shorter events, 0.0 us)
Async XLA Ops:
  0.6 5.6 %copy-start.1 = (s32[128]{0:T(128)S(1)}, s32[128]{0:T(128)}, u32[]{:S(2)}) copy-start(s32[128]{0:T(128)} %param.13) | copy-start | bytes 1540
  90.8 8.3 %copy-start = (f32[8192]{0:T(1024)}, f32[8192]{0:T(1024)S(1)}, u32[]{:S(2)}) copy-start(f32[8192]{0:T(1024)S(1)} %log_add_fusion) | copy-start | bytes 98308

commit v2 on v1

--- a/solution.py
+++ b/solution.py
@@ -78,21 +78,26 @@
 
         def row_block(ib, c):
             row = ib * edge
-            for i in range(edge):
-                f = [factors[element(m * n + row + i), :] for m in range(edge)]
+            start = 0
+            for size in (edge - edge // 2, edge // 2):
+                rows = range(start, start + size)
+                start += size
+                f = [[factors[element(m * n + row + i), :] for m in range(edge)] for i in rows]
                 for j in range(edge):
-                    total = f[j]
+                    totals = [f[a][j] for a in range(size)]
                     for m in range(j + 1, edge):
-                        total = total + f[m] * inverse[m][j]
-                    table[at(row + i, first + j), :] = -total
-
-            for i in range(edge):
-                f = [factors[element(m * n + row + i), :] for m in range(edge)]
-                for j in range(i, edge):
-                    value = table[at(row + i, row + j), :]
+                        v = table[at(first + m, first + j), :]
+                        totals = [totals[a] + f[a][m] * v for a in range(size)]
+                    for a, i in enumerate(rows):
+                        table[at(row + i, first + j), :] = -totals[a]
+                for j in range(rows[0], edge):
+                    live = [a for a, i in enumerate(rows) if i <= j]
+                    values = [table[at(row + rows[a], row + j), :] for a in live]
                     for m in range(edge):
-                        value = value - f[m] * table[at(first + m, row + j), :]
-                    table[at(row + i, row + j), :] = value
+                        u = table[at(first + m, row + j), :]
+                        values = [v - f[a][m] * u for a, v in zip(live, values)]
+                    for a, v in zip(live, values):
+                        table[at(row + rows[a], row + j), :] = v
 
             def full(index, cc):
                 jb = jnp.where(index < kb, index, index - kb + ib + 1)
@@ -131,15 +136,18 @@
 
 
 def main_kernel(
-    n, tiles, patterns,
-    index_ref, effects_ref, se_ref, covar_ref, prior_ref,
-    out_ref, max_ref, sum_ref,
-    table, pivots, factors, roots, halfdet, noise, weights, flipped, stack, acc, se_rows,
+    n, tiles, patterns, grids,
+    index_ref, grid_ref, effects_hbm, se_ref, covar_ref, comp_grid_ref, prior_ref,
+    out_hbm, peak_ref,
+    table, pivots, factors, roots, halfdet, noise, weights, effects_ref, flipped, following, stack, acc, done, out_buf, se_rows,
+    in_sem, out_sem,
     count_s, start_s, slot_s, order_s,
 ):
-    comps = LANES
     even = n // 16 * 16
     edge_rows = n - even
+    edge = block_edge(n)
+    fetch = pltpu.make_async_copy(effects_hbm, effects_ref, in_sem)
+    fetch.start()
 
     def clear(b, c):
         count_s[b] = 0
@@ -173,9 +181,44 @@
         return c
 
     lax.fori_loop(0, tiles, sort, 0)
+    order_s[tiles] = 0
 
     weights[...] = jnp.zeros_like(weights)
     stack[...] = jnp.zeros_like(stack)
+    chosen = comp_grid_ref[...]
+    scale = jnp.zeros(chosen.shape, jnp.float32)
+    for g in range(grids):
+        scale = jnp.where(chosen == g, grid_ref[g], scale)
+    scale = jnp.broadcast_to(scale * scale, (SUB, LANES))
+    log_prior = jnp.log(prior_ref[...]) - 0.5 * n * math.log(2.0 * math.pi)
+
+    def columns(t):
+        return pl.ds(pl.multiple_of(t * TILE, TILE), TILE)
+
+    def prepare(t, target):
+        at = columns(t)
+        data = effects_ref[pl.ds(0, even), at]
+        x1, x2, x3 = split3(data)
+        for piece, part in enumerate((x1, x2, x1, x2, x3)):
+            stack[pl.ds(piece * even, even), :] = part.astype(jnp.float32)
+        for extra in range(edge_rows):
+            line = effects_ref[pl.ds(even + extra, 1), at]
+            x1, x2, x3 = split3(line)
+            for piece, part in enumerate((x1, x2, x1, x2, x3)):
+                stack[pl.ds(PIECES * even + extra * PIECES + piece, 1), :] = part.astype(jnp.float32)
+        target[...] = jnp.transpose(stack[...]).astype(jnp.bfloat16)
+
+    def conclude(t, side):
+        at = columns(t)
+        scores = jnp.transpose(done[...])
+        top = jnp.max(scores, axis=0, keepdims=True)
+        shifted = jnp.exp(scores - top)
+        out_buf[side] = shifted
+        peak_ref[0:1, at] = top
+        peak_ref[1:2, at] = jnp.sum(shifted, axis=0, keepdims=True)
+
+    def store(t, side):
+        return pltpu.make_async_copy(out_buf.at[side], out_hbm.at[:, columns(t)], out_sem.at[side])
 
     def one_batch(batch, carry):
         base = batch * SUB
@@ -187,30 +230,28 @@
         for i in range(n):
             noise[pl.ds(i * SUB, SUB), :] = jnp.broadcast_to(squares[:, i : i + 1], (SUB, LANES))
 
-        def fill_row(i, c):
-            def fill(j, cc):
-                e = i * n + j
-                table[element(e), :] = covar_ref[pl.ds(e, SUB, stride=0), :]
-                return cc
-
-            def fill_block(jb, cc):
-                for a in range(block_edge(n)):
-                    fill(jb * block_edge(n) + a, 0)
-                return cc
-
-            lax.fori_loop(i // block_edge(n), n // block_edge(n), fill_block, 0)
-            d = element(i * n + i)
-            table[d, :] = table[d, :] + noise[element(i), :]
-            return c
-
-        lax.fori_loop(0, n, fill_row, 0)
+        for rb in range(n // edge):
+            def fill_row(i, c):
+                for j in range(rb * edge, n):
+                    e = i * n + j
+                    table[element(e), :] = covar_ref[pl.ds(e, SUB, stride=0), :] * scale
+                d = element(i * n + i)
+                table[d, :] = table[d, :] + noise[element(i), :]
+                return c
+
+            lax.fori_loop(rb * edge, (rb + 1) * edge, fill_row, 0)
         eliminate(n, table, pivots, factors)
         logs = jnp.zeros((SUB, LANES), jnp.float32)
         for i in range(n):
             d = pivots[pl.ds(i * SUB, SUB), :]
             roots[pl.ds(i * SUB, SUB), :] = lax.rsqrt(d)
             logs = logs + jnp.log(d)
-        halfdet[...] = prior_ref[...] - 0.5 * logs
+        halfdet[...] = log_prior - 0.5 * logs
+
+        @pl.when(batch == 0)
+        def _():
+            fetch.wait()
+            prepare(order_s[0], following)
 
         def one_slot(slot, c):
             s = slot - base
@@ -238,18 +279,16 @@
             row_const = halfdet[pl.ds(s, 1), :]
 
             def one_tile(place_at, cc):
-                t = order_s[place_at]
-                at = pl.ds(pl.multiple_of(t * TILE, TILE), TILE)
-                data = effects_ref[pl.ds(0, even), at]
-                x1, x2, x3 = split3(data)
-                for piece, part in enumerate((x1, x2, x1, x2, x3)):
-                    stack[pl.ds(piece * even, even), :] = part.astype(jnp.float32)
-                for extra in range(edge_rows):
-                    line = effects_ref[pl.ds(even + extra, 1), at]
-                    x1, x2, x3 = split3(line)
-                    for piece, part in enumerate((x1, x2, x1, x2, x3)):
-                        stack[pl.ds(PIECES * even + extra * PIECES + piece, 1), :] = part.astype(jnp.float32)
-                flipped[...] = jnp.transpose(stack[...]).astype(jnp.bfloat16)
+                before = order_s[jnp.maximum(place_at - 1, 0)]
+                side = lax.rem(place_at, 2)
+
+                @pl.when(place_at >= 3)
+                def _():
+                    store(0, 1 - side).wait()
+
+                flipped[...] = following[...]
+                prepare(order_s[place_at + 1], following)
+                conclude(before, 1 - side)
                 for i in range(0, n, 2):
                     if i + 1 < n:
                         right = jnp.concatenate([weights[i], weights[i + 1]], axis=1)
@@ -263,12 +302,12 @@
                         acc[...] += square
                     else:
                         acc[...] = square
-                scores = jnp.transpose(row_const - 0.5 * acc[...])
-                top = jnp.max(scores, axis=0, keepdims=True)
-                shifted = jnp.exp(scores - top)
-                out_ref[:, at] = shifted
-                max_ref[:, at] = top
-                sum_ref[:, at] = jnp.sum(shifted, axis=0, keepdims=True)
+                done[...] = row_const - 0.5 * acc[...]
+
+                @pl.when(place_at >= 1)
+                def _():
+                    store(before, 1 - side).start()
+
                 return cc
 
             lax.fori_loop(start_s[slot], start_s[slot + 1], one_tile, 0)
@@ -278,29 +317,37 @@
         return carry
 
     lax.fori_loop(0, (used + SUB - 1) // SUB, one_batch, 0)
-
-
-def shifted_scores(effects, se_table, se_index, covar, prior):
+    last = order_s[tiles - 1]
+    side = (tiles - 1) % 2
+    if tiles >= 3:
+        store(0, side).wait()
+    conclude(last, side)
+    store(last, side).start()
+    if tiles >= 2:
+        store(0, 1 - side).wait()
+    store(last, side).wait()
+
+
+def shifted_scores(effects, se_table, se_index, covar, grid_scale, comp_grid, weights):
     n, pairs = effects.shape
     patterns = se_table.shape[0]
     tiles = pairs // TILE
     even = n // 16 * 16
     assert covar.shape == (n * n, LANES) and (n - even) * PIECES <= 16
     depth = PIECES * even + 16
-    se_wide = jnp.pad(se_table, ((0, 0), (0, LANES - n)))
     vmem = pl.BlockSpec(memory_space=pltpu.VMEM)
     smem = pl.BlockSpec(memory_space=pltpu.SMEM)
+    hbm = pl.BlockSpec(memory_space=pl.ANY)
     f32 = jnp.float32
     return pl.pallas_call(
-        functools.partial(main_kernel, n, tiles, patterns),
+        functools.partial(main_kernel, n, tiles, patterns, grid_scale.shape[0]),
         name="shifted_scores",
         out_shape=(
             jax.ShapeDtypeStruct((LANES, pairs), f32),
-            jax.ShapeDtypeStruct((1, pairs), f32),
-            jax.ShapeDtypeStruct((1, pairs), f32),
+            jax.ShapeDtypeStruct((2, pairs), f32),
         ),
-        in_specs=[smem, vmem, vmem, vmem, vmem],
-        out_specs=(vmem, vmem, vmem),
+        in_specs=[smem, smem, hbm, vmem, vmem, vmem, vmem],
+        out_specs=(hbm, vmem),
         scratch_shapes=[
             pltpu.VMEM((n * n * SUB, LANES), f32),
             pltpu.VMEM((n * SUB, LANES), f32),
@@ -309,36 +356,58 @@
             pltpu.VMEM((SUB, LANES), f32),
             pltpu.VMEM((n * SUB, LANES), f32),
             pltpu.VMEM((n, depth, LANES), jnp.bfloat16),
+            pltpu.VMEM((n, pairs), f32),
+            pltpu.VMEM((TILE, depth), jnp.bfloat16),
             pltpu.VMEM((TILE, depth), jnp.bfloat16),
             pltpu.VMEM((depth, TILE), f32),
             pltpu.VMEM((TILE, LANES), f32),
-            pltpu.VMEM((SUB, LANES), f32),
+            pltpu.VMEM((TILE, LANES), f32),
+            pltpu.VMEM((2, LANES, TILE), f32),
+            pltpu.VMEM((SUB, n), f32),
+            pltpu.SemaphoreType.DMA,
+            pltpu.SemaphoreType.DMA((2,)),
             pltpu.SMEM((patterns + 1,), jnp.int32),
             pltpu.SMEM((patterns + 1,), jnp.int32),
             pltpu.SMEM((patterns + 1,), jnp.int32),
-            pltpu.SMEM((tiles,), jnp.int32),
+            pltpu.SMEM((tiles + 1,), jnp.int32),
         ],
-        compiler_params=pltpu.CompilerParams(vmem_limit_bytes=60 * 1024 * 1024),
-    )(se_index, effects, se_wide, covar, prior)
+        compiler_params=pltpu.CompilerParams(vmem_limit_bytes=48 * 1024 * 1024),
+    )(se_index, grid_scale, effects, se_table, covar, comp_grid[None], weights[None])
 
 
 def exact_dot(left, right, dims):
     return lax.dot_general(left, right, (dims, ((), ())), precision=lax.Precision.HIGHEST, preferred_element_type=jnp.float32)
 
 
-def finish_kernel(shifted_ref, scale_ref, out_ref, mass_ref):
-    value = shifted_ref[...] * scale_ref[...]
+def finish_kernel(shifted_ref, own_ref, peaks_ref, out_ref, loglik_ref, mass_ref, partial):
+    tops = [peaks_ref[c, 0:1, :] for c in range(peaks_ref.shape[0])]
+    sums = [peaks_ref[c, 1:2, :] for c in range(peaks_ref.shape[0])]
+    top = functools.reduce(jnp.maximum, tops)
+    total = sum(s * jnp.exp(t - top) for s, t in zip(sums, tops))
+    loglik = top + jnp.log(total)
+    loglik_ref[...] = loglik
+    value = shifted_ref[...] * jnp.exp(own_ref[0:1, :] - loglik)
     out_ref[...] = value
-    total = jnp.sum(value, axis=1, keepdims=True)
-
-    @pl.when(pl.program_id(0) == 0)
+    chunk = value[:, :LANES]
+    for c in range(1, value.shape[1] // LANES):
+        chunk = chunk + value[:, c * LANES : (c + 1) * LANES]
+    step = pl.program_id(0)
+
+    @pl.when(step == 0)
     def _():
-        mass_ref[...] = jnp.zeros_like(mass_ref)
-
-    mass_ref[...] += total
-
-
-def finish(shifted, scale):
+        partial[...] = chunk
+
+    @pl.when(step > 0)
+    def _():
+        partial[...] += chunk
+
+    @pl.when(step == pl.num_programs(0) - 1)
+    def _():
+        mass = jnp.sum(jnp.transpose(partial[...]), axis=0, keepdims=True)
+        mass_ref[...] = jnp.broadcast_to(mass, mass_ref.shape)
+
+
+def finish(shifted, peak, peaks, receivers):
     comps, pairs = shifted.shape
     width = min(pairs, 1024)
     return pl.pallas_call(
@@ -347,17 +416,21 @@
         grid=(pairs // width,),
         in_specs=[
             pl.BlockSpec((comps, width), lambda g: (0, g)),
-            pl.BlockSpec((1, width), lambda g: (0, g)),
+            pl.BlockSpec((2, width), lambda g: (0, g)),
+            pl.BlockSpec((peaks.shape[0], 2, width), lambda g: (0, 0, g)),
         ],
         out_specs=(
             pl.BlockSpec((comps, width), lambda g: (0, g)),
-            pl.BlockSpec((comps, 1), lambda g: (0, 0)),
+            pl.BlockSpec((1, width), lambda g: (0, g)),
+            pl.BlockSpec((receivers, comps), lambda g: (0, 0)),
         ),
         out_shape=(
             jax.ShapeDtypeStruct((comps, pairs), jnp.float32),
-            jax.ShapeDtypeStruct((comps, 1), jnp.float32),
+            jax.ShapeDtypeStruct((1, pairs), jnp.float32),
+            jax.ShapeDtypeStruct((receivers, comps), jnp.float32),
         ),
-    )(shifted, scale)
+        scratch_shapes=[pltpu.VMEM((LANES, LANES), jnp.float32)],
+    )(shifted, peak, peaks)
 
 
 def per_device(effects, se_table, se_index, base_root, grid_scale, comp_base, comp_grid, weights):
@@ -366,23 +439,17 @@
     covariances = jnp.einsum("uij,ukj->uik", base_root, base_root, precision=lax.Precision.HIGHEST)
     covariances = covariances.reshape(covariances.shape[0], n * n)
     bases = jnp.arange(covariances.shape[0], dtype=jnp.int32)
-    grids = jnp.arange(grid_scale.shape[0], dtype=jnp.int32)
-    scale = jnp.sum(jnp.where(comp_grid[None] == grids[:, None], grid_scale[:, None], 0.0), axis=0)
     pick = (comp_base[None] == bases[:, None]).astype(jnp.float32)
-    covar = exact_dot(covariances, pick, ((0,), (0,))) * (scale * scale)[None]
-    prior = (jnp.log(weights) - 0.5 * n * math.log(2.0 * math.pi))[None]
-    shifted, top, total = shifted_scores(effects, se_table, se_index, covar, prior)
-    both = lax.all_gather(jnp.concatenate([top, total], axis=0), "comp")
-    tops, totals = both[:, 0], both[:, 1]
-    score_max = jnp.max(tops, axis=0)
-    score_sum = jnp.sum(totals * jnp.exp(tops - score_max), axis=0)
-    pair_loglik = score_max + jnp.log(score_sum)
-    responsibility, mass = finish(shifted, jnp.exp(top - pair_loglik[None]))
-    masses = lax.psum(mass[:, 0], "pairs")
+    covar = exact_dot(covariances, pick, ((0,), (0,)))
+    shifted, peak = shifted_scores(effects, se_table, se_index, covar, grid_scale, comp_grid, weights)
+    peaks = lax.all_gather(peak, "comp")
+    receivers = lax.axis_size("pairs")
+    responsibility, loglik, mass = finish(shifted, peak, peaks, receivers)
+    masses = jnp.sum(lax.all_to_all(mass, "pairs", 0, 0, tiled=True), axis=0)
     all_pairs = pairs * lax.axis_size("pairs")
     all_comps = comps * lax.axis_size("comp")
     log_weights = jnp.log((masses + 1.0) / (all_pairs + all_comps))
-    return (responsibility, log_weights, pair_loglik)
+    return (responsibility, log_weights, loglik[0])
 
 
 def solution(mesh):

time: 145 us -> 96.7 us (0.67)
  blocking collectives: 45.6 us -> 17.4 us
  Pallas kernels: 86 us -> 73 us
  other arithmetic: 6 us -> 0.56 us
    psum x1 -> x0, blocking collectives: 43.6 us -> none  [per_device(): masses = lax.psum(mass[:, 0], 'pairs')]
    all_to_all x0 -> x1, blocking collectives: none -> 15.3 us  [per_device(): masses = jnp.sum(lax.all_to_all(mass, 'pairs', 0, 0, tiled=True), axis=0)]
    pallas_call x1, Pallas kernels: 79.1 us -> 66 us  [shifted_scores(): pl.pallas_call(functools.partial(main_kernel, n, tiles, patterns, grid_sc...]
where the time goes in v2:
time: 96.7 us; the launch traced here: 96.1 us
  Pallas kernels  73 us (75%)
  blocking collectives  17.4 us (18%)
  matrix products  4.15 us (4%)
    pallas_call x1, Pallas kernels, shifted_scores(): pl.pallas_call(functools.partial(main_kernel, n, tiles, patterns, grid_sc...  66 us
    all_to_all x1, blocking collectives, per_device(): masses = jnp.sum(lax.all_to_all(mass, 'pairs', 0, 0, tiled=True), axis=0)  15.3 us
    pallas_call x1, Pallas kernels, finish(): pl.pallas_call(finish_kernel, name='finish', grid=(pairs // width,), in_s...  6.99 us
    dot_general x1, matrix products, per_device(): jnp.einsum('uij,ukj->uik', base_root, base_root, precision=lax.Precision....  2.33 us
    all_gather x1, blocking collectives, per_device(): peaks = lax.all_gather(peak, 'comp')  2.17 us

profile of v2, /device:TPU:0, one launch (start us, length us, event | category | flops | bytes accessed | tf_op | source)
XLA Modules:
  0.0 96.1 jit_solution(13208283707352891053)
XLA Ops:
  0.6 0.0 copy-start.6
  0.6 0.0 copy-start.5
  0.7 0.0 copy-start.4
  0.7 0.0 copy-start.3
  0.7 0.0 copy-start.2
  0.7 0.0 copy-start
  0.7 2.3 %fusion = f32[16,49,49]{2,1,0:T(8,128)S(1)} fusion(f32[16,49,49]{2,0,1:T(8,128)} %param.11), kind=kOutput, calls=%fused_computation | convolution fusion | flops 22588608 | bytes 307328 | tf_op jit(solution)/shard_map/uij,ukj->uik/dot_general | solution.py:439
  3.0 0.2 reshape.12
  3.2 1.8 %fusion.2.covar_ref = f32[2401,128]{1,0:T(8,128)S(1)} fusion(f32[16,2401]{1,0:T(8,128)S(1)} %reshape.12, s32[128]{0:T(128)} %param.13), kind=kOutput, calls=%fused_computation.3 | convolution fusion | flops 59009024 | bytes 1383488 | tf_op jit(solution)/shard_map/dot_general | solution.py:379
  5.0 0.0 copy-done.6
  5.0 0.0 copy-done.5
  5.0 0.0 copy-done.4
  5.1 0.0 copy-done.3
  5.1 0.0 copy-done.2
  5.1 0.0 copy-done
  5.1 66.0 %shifted_scores.1 = (f32[128,8192]{1,0:T(8,128)}, f32[2,8192]{1,0:T(2,128)S(1)}) custom-call(s32[16]{0:T(128)S(1)} %copy-done.3, f32[16]{0:T(128)S(1)} %copy-done.4, f32[49,8192]{1,0:T(8,128)S(1)} %copy-done, f32[16,49]{1,0:T(8,128)S(1)} %copy-done.2, f32[2401,128]{1,0:T(8,128)S(1)} %fusion.2.covar_ref, s32[1,128]{1,0:T(1,128)S(1)} %bitcast.9, ...), custom_call_target="tpu_custom_call" | custom-call | tf_op jit(solution)/shard_map/shifted_scores/pallas_call | solution.py:342
  71.1 0.0 copy-start.1
  71.1 2.2 %all-gather.1.peaks_ref = f32[2,2,8192]{2,1,0:T(2,128)} all-gather(f32[1,2,8192]{2,1,0:T(2,128)S(1)} %bitcast.8), channel_id=2, replica_groups=mesh['pairs'=16,'comp'=2] {'comp'}, dimensions={0}, use_global_device_ids=true | all-gather | bytes 196608 | tf_op jit(solution)/shard_map/all_gather | solution.py:445
  73.3 0.0 copy-done.1
  73.3 7.0 %finish.1 = (f32[128,8192]{1,0:T(8,128)}, f32[1,8192]{1,0:T(1,128)}, f32[16,128]{1,0:T(8,128)}) custom-call(f32[128,8192]{1,0:T(8,128)} %get-tuple-element.8.shifted_ref, f32[2,8192]{1,0:T(2,128)} %copy-done.1, f32[2,2,8192]{2,1,0:T(2,128)} %all-gather.1.peaks_ref), custom_call_target="tpu_custom_call" | custom-call | tf_op jit(solution)/shard_map/finish/pallas_call | solution.py:413
  80.3 15.3 %all_to_all.9 = f32[16,1,128]{2,1,0:T(1,128)S(1)} all-to-all(f32[16,1,128]{2,1,0:T(1,128)} %bitcast.11), channel_id=1, replica_groups=mesh['pairs'=16,'comp'=2] {'pairs'}, dimensions={0} | all-to-all | bytes 16384 | tf_op jit(solution)/shard_map/all_to_all | solution.py:448
  95.6 0.5 multiply_log_fusion
  (1 shorter events, 0.0 us)
Async XLA Ops:
  0.6 4.4 %copy-start.6 = (f32[128]{0:T(128)S(1)}, f32[128]{0:T(128)}, u32[]{:S(2)}) copy-start(f32[128]{0:T(128)} %param.15) | copy-start | bytes 1540
  0.6 4.4 %copy-start.5 = (s32[128]{0:T(128)S(1)}, s32[128]{0:T(128)}, u32[]{:S(2)}) copy-start(s32[128]{0:T(128)} %param.14) | copy-start | bytes 1540
  0.7 4.4 %copy-start.4 = (f32[16]{0:T(128)S(1)}, f32[16]{0:T(128)}, u32[]{:S(2)}) copy-start(f32[16]{0:T(128)} %grid_ref.1) | copy-start | bytes 196
  0.7 4.4 %copy-start.3 = (s32[16]{0:T(128)S(1)}, s32[16]{0:T(128)}, u32[]{:S(2)}) copy-start(s32[16]{0:T(128)} %index_ref.1) | copy-start | bytes 196
  0.7 4.4 %copy-start.2 = (f32[16,49]{1,0:T(8,128)S(1)}, f32[16,49]{1,0:T(8,128)}, u32[]{:S(2)}) copy-start(f32[16,49]{1,0:T(8,128)} %se_ref.1) | copy-start | bytes 9412
  0.7 4.4 %copy-start = (f32[49,8192]{1,0:T(8,128)S(1)}, f32[49,8192]{1,0:T(8,128)}, u32[]{:S(2)}) copy-start(f32[49,8192]{1,0:T(8,128)} %effects_hbm.1) | copy-start | bytes 4816900
  71.1 2.2 %copy-start.1 = (f32[2,8192]{1,0:T(2,128)}, f32[2,8192]{1,0:T(2,128)S(1)}, u32[]{:S(2)}) copy-start(f32[2,8192]{1,0:T(2,128)S(1)} %get-tuple-element.9.own_ref) | copy-start | bytes 196612

commit v3 on v2

--- a/solution.py
+++ b/solution.py
@@ -137,10 +137,10 @@
 
 def main_kernel(
     n, tiles, patterns, grids,
-    index_ref, grid_ref, effects_hbm, se_ref, covar_ref, comp_grid_ref, prior_ref,
+    index_ref, grid_ref, effects_hbm, se_ref, covar_hbm, comp_grid_ref, prior_ref,
     out_hbm, peak_ref,
-    table, pivots, factors, roots, halfdet, noise, weights, effects_ref, flipped, following, stack, acc, done, out_buf, se_rows,
-    in_sem, out_sem,
+    table, pivots, factors, roots, halfdet, noise, weights, effects_ref, covar_ref, flipped, following, stack, acc, done, out_buf, se_rows,
+    in_sem, covar_sem, out_sem,
     count_s, start_s, slot_s, order_s,
 ):
     even = n // 16 * 16
@@ -148,6 +148,8 @@
     edge = block_edge(n)
     fetch = pltpu.make_async_copy(effects_hbm, effects_ref, in_sem)
     fetch.start()
+    fetch_covar = pltpu.make_async_copy(covar_hbm, covar_ref, covar_sem)
+    fetch_covar.start()
 
     def clear(b, c):
         count_s[b] = 0
@@ -191,6 +193,8 @@
         scale = jnp.where(chosen == g, grid_ref[g], scale)
     scale = jnp.broadcast_to(scale * scale, (SUB, LANES))
     log_prior = jnp.log(prior_ref[...]) - 0.5 * n * math.log(2.0 * math.pi)
+
+    fetch_covar.wait()
 
     def columns(t):
         return pl.ds(pl.multiple_of(t * TILE, TILE), TILE)
@@ -346,7 +350,7 @@
             jax.ShapeDtypeStruct((LANES, pairs), f32),
             jax.ShapeDtypeStruct((2, pairs), f32),
         ),
-        in_specs=[smem, smem, hbm, vmem, vmem, vmem, vmem],
+        in_specs=[smem, smem, hbm, vmem, hbm, vmem, vmem],
         out_specs=(hbm, vmem),
         scratch_shapes=[
             pltpu.VMEM((n * n * SUB, LANES), f32),
@@ -357,6 +361,7 @@
             pltpu.VMEM((n * SUB, LANES), f32),
             pltpu.VMEM((n, depth, LANES), jnp.bfloat16),
             pltpu.VMEM((n, pairs), f32),
+            pltpu.VMEM((n * n, LANES), f32),
             pltpu.VMEM((TILE, depth), jnp.bfloat16),
             pltpu.VMEM((TILE, depth), jnp.bfloat16),
             pltpu.VMEM((depth, TILE), f32),
@@ -365,13 +370,14 @@
             pltpu.VMEM((2, LANES, TILE), f32),
             pltpu.VMEM((SUB, n), f32),
             pltpu.SemaphoreType.DMA,
+            pltpu.SemaphoreType.DMA,
             pltpu.SemaphoreType.DMA((2,)),
             pltpu.SMEM((patterns + 1,), jnp.int32),
             pltpu.SMEM((patterns + 1,), jnp.int32),
             pltpu.SMEM((patterns + 1,), jnp.int32),
             pltpu.SMEM((tiles + 1,), jnp.int32),
         ],
-        compiler_params=pltpu.CompilerParams(vmem_limit_bytes=48 * 1024 * 1024),
+        compiler_params=pltpu.CompilerParams(vmem_limit_bytes=26 * 1024 * 1024),
     )(se_index, grid_scale, effects, se_table, covar, comp_grid[None], weights[None])
 
 
@@ -379,57 +385,50 @@
     return lax.dot_general(left, right, (dims, ((), ())), precision=lax.Precision.HIGHEST, preferred_element_type=jnp.float32)
 
 
-def finish_kernel(shifted_ref, own_ref, peaks_ref, out_ref, loglik_ref, mass_ref, partial):
-    tops = [peaks_ref[c, 0:1, :] for c in range(peaks_ref.shape[0])]
-    sums = [peaks_ref[c, 1:2, :] for c in range(peaks_ref.shape[0])]
-    top = functools.reduce(jnp.maximum, tops)
-    total = sum(s * jnp.exp(t - top) for s, t in zip(sums, tops))
-    loglik = top + jnp.log(total)
-    loglik_ref[...] = loglik
-    value = shifted_ref[...] * jnp.exp(own_ref[0:1, :] - loglik)
-    out_ref[...] = value
-    chunk = value[:, :LANES]
-    for c in range(1, value.shape[1] // LANES):
-        chunk = chunk + value[:, c * LANES : (c + 1) * LANES]
-    step = pl.program_id(0)
-
-    @pl.when(step == 0)
-    def _():
-        partial[...] = chunk
-
-    @pl.when(step > 0)
-    def _():
-        partial[...] += chunk
-
-    @pl.when(step == pl.num_programs(0) - 1)
-    def _():
-        mass = jnp.sum(jnp.transpose(partial[...]), axis=0, keepdims=True)
-        mass_ref[...] = jnp.broadcast_to(mass, mass_ref.shape)
+def finish_kernel(width, shifted_ref, own_ref, peaks_ref, out_hbm, loglik_ref, mass_ref, buffer, sems):
+    pairs = shifted_ref.shape[1]
+    steps = pairs // width
+    copies = []
+    partial = None
+    for step in range(steps):
+        at = pl.ds(step * width, width)
+        tops = [peaks_ref[c, 0:1, at] for c in range(peaks_ref.shape[0])]
+        sums = [peaks_ref[c, 1:2, at] for c in range(peaks_ref.shape[0])]
+        top = functools.reduce(jnp.maximum, tops)
+        total = sum(s * jnp.exp(t - top) for s, t in zip(sums, tops))
+        loglik = top + jnp.log(total)
+        loglik_ref[:, at] = loglik
+        factor = jnp.exp(own_ref[0:1, at] - loglik)
+        for c in range(width // LANES):
+            lanes = pl.ds(step * width + c * LANES, LANES)
+            value = shifted_ref[:, lanes] * factor[:, c * LANES : (c + 1) * LANES]
+            buffer[:, lanes] = value
+            partial = value if partial is None else partial + value
+        copy = pltpu.make_async_copy(buffer.at[:, at], out_hbm.at[:, at], sems.at[step])
+        copy.start()
+        copies.append(copy)
+    mass = jnp.sum(jnp.transpose(partial), axis=0, keepdims=True)
+    mass_ref[...] = jnp.broadcast_to(mass, mass_ref.shape)
+    for copy in copies:
+        copy.wait()
 
 
 def finish(shifted, peak, peaks, receivers):
     comps, pairs = shifted.shape
     width = min(pairs, 1024)
+    vmem = pl.BlockSpec(memory_space=pltpu.VMEM)
     return pl.pallas_call(
-        finish_kernel,
+        functools.partial(finish_kernel, width),
         name="finish",
-        grid=(pairs // width,),
-        in_specs=[
-            pl.BlockSpec((comps, width), lambda g: (0, g)),
-            pl.BlockSpec((2, width), lambda g: (0, g)),
-            pl.BlockSpec((peaks.shape[0], 2, width), lambda g: (0, 0, g)),
-        ],
-        out_specs=(
-            pl.BlockSpec((comps, width), lambda g: (0, g)),
-            pl.BlockSpec((1, width), lambda g: (0, g)),
-            pl.BlockSpec((receivers, comps), lambda g: (0, 0)),
-        ),
+        in_specs=[vmem, vmem, vmem],
+        out_specs=(pl.BlockSpec(memory_space=pl.ANY), vmem, vmem),
         out_shape=(
             jax.ShapeDtypeStruct((comps, pairs), jnp.float32),
             jax.ShapeDtypeStruct((1, pairs), jnp.float32),
             jax.ShapeDtypeStruct((receivers, comps), jnp.float32),
         ),
-        scratch_shapes=[pltpu.VMEM((LANES, LANES), jnp.float32)],
+        scratch_shapes=[pltpu.VMEM((comps, pairs), jnp.float32), pltpu.SemaphoreType.DMA((pairs // width,))],
+        compiler_params=pltpu.CompilerParams(vmem_limit_bytes=12 * 1024 * 1024),
     )(shifted, peak, peaks)
 
 

time: 96.7 us -> 92.1 us (0.952)
  Pallas kernels: 73 us -> 52.9 us
  blocking collectives: 17.4 us -> 33.2 us
    pallas_call x1, Pallas kernels: 66 us -> 49.8 us  [shifted_scores(): pl.pallas_call(functools.partial(main_kernel, n, tiles, patterns, grid_sc...]
    all_to_all x1, blocking collectives: 15.3 us -> 31.2 us  [per_device(): masses = jnp.sum(lax.all_to_all(mass, 'pairs', 0, 0, tiled=True), axis=0)]
    pallas_call x1, Pallas kernels: 6.99 us -> 3.12 us  [finish(): pl.pallas_call(functools.partial(finish_kernel, width), name='finish', in...]
where the time goes in v3:
time: 92.1 us; the launch traced here: 91.8 us
  Pallas kernels  52.9 us (57%)
  blocking collectives  33.2 us (36%)
  matrix products  4.15 us (5%)
    pallas_call x1, Pallas kernels, shifted_scores(): pl.pallas_call(functools.partial(main_kernel, n, tiles, patterns, grid_sc...  49.8 us
    all_to_all x1, blocking collectives, per_device(): masses = jnp.sum(lax.all_to_all(mass, 'pairs', 0, 0, tiled=True), axis=0)  31.2 us
    pallas_call x1, Pallas kernels, finish(): pl.pallas_call(functools.partial(finish_kernel, width), name='finish', in...  3.12 us
    dot_general x1, matrix products, per_device(): jnp.einsum('uij,ukj->uik', base_root, base_root, precision=lax.Precision....  2.33 us
    all_gather x1, blocking collectives, per_device(): peaks = lax.all_gather(peak, 'comp')  2.04 us

profile of v3, /device:TPU:0, one launch (start us, length us, event | category | flops | bytes accessed | tf_op | source)
XLA Modules:
  0.0 91.8 jit_solution(8911417660644878499)
XLA Ops:
  0.6 0.0 copy-start.5
  0.6 0.0 copy-start.4
  0.7 0.0 copy-start.3
  0.7 0.0 copy-start.2
  0.7 0.0 copy-start.1
  0.7 0.0 copy-start
  0.7 2.3 %fusion = f32[16,49,49]{2,1,0:T(8,128)S(1)} fusion(f32[16,49,49]{2,0,1:T(8,128)} %param.11), kind=kOutput, calls=%fused_computation | convolution fusion | flops 22588608 | bytes 307328 | tf_op jit(solution)/shard_map/uij,ukj->uik/dot_general | solution.py:438
  3.0 0.2 reshape.12
  3.2 1.8 %fusion.2.covar_hbm = f32[2401,128]{1,0:T(8,128)S(1)} fusion(f32[16,2401]{1,0:T(8,128)S(1)} %reshape.12, s32[128]{0:T(128)} %param.13), kind=kOutput, calls=%fused_computation.3 | convolution fusion | flops 59009024 | bytes 1383488 | tf_op jit(solution)/shard_map/dot_general | solution.py:385
  5.0 0.0 copy-done.5
  5.0 0.0 copy-done.4
  5.0 0.0 copy-done.3
  5.1 0.0 copy-done.2
  5.1 0.0 copy-done.1
  5.1 0.0 copy-done
  5.1 49.8 %shifted_scores.1 = (f32[128,8192]{1,0:T(8,128)S(1)}, f32[2,8192]{1,0:T(2,128)S(1)}) custom-call(s32[16]{0:T(128)S(1)} %copy-done.2, f32[16]{0:T(128)S(1)} %copy-done.3, f32[49,8192]{1,0:T(8,128)S(1)} %copy-done, f32[16,49]{1,0:T(8,128)S(1)} %copy-done.1, f32[2401,128]{1,0:T(8,128)S(1)} %fusion.2.covar_hbm, s32[1,128]{1,0:T(1,128)S(1)} %bitcast.10, ...), custom_call_target="tpu_custom_call" | custom-call | tf_op jit(solution)/shard_map/shifted_scores/pallas_call | solution.py:346
  54.9 2.0 %all-gather.1.peaks_ref = f32[2,2,8192]{2,1,0:T(2,128)S(1)} all-gather(f32[1,2,8192]{2,1,0:T(2,128)S(1)} %bitcast.8), channel_id=2, replica_groups=mesh['pairs'=16,'comp'=2] {'comp'}, dimensions={0}, use_global_device_ids=true | all-gather | bytes 196608 | tf_op jit(solution)/shard_map/all_gather | solution.py:444
  56.9 3.1 %finish.1 = (f32[128,8192]{1,0:T(8,128)}, f32[1,8192]{1,0:T(1,128)}, f32[16,128]{1,0:T(8,128)S(1)}) custom-call(f32[128,8192]{1,0:T(8,128)S(1)} %get-tuple-element.8.shifted_ref, f32[2,8192]{1,0:T(2,128)S(1)} %get-tuple-element.9.own_ref, f32[2,2,8192]{2,1,0:T(2,128)S(1)} %all-gather.1.peaks_ref), custom_call_target="tpu_custom_call" | custom-call | tf_op jit(solution)/shard_map/finish/pallas_call | solution.py:420
  60.1 31.2 %all_to_all.9 = f32[16,1,128]{2,1,0:T(1,128)S(1)} all-to-all(f32[16,1,128]{2,1,0:T(1,128)S(1)} %bitcast.9), channel_id=1, replica_groups=mesh['pairs'=16,'comp'=2] {'pairs'}, dimensions={0} | all-to-all | bytes 16384 | tf_op jit(solution)/shard_map/all_to_all | solution.py:447
  91.3 0.5 multiply_log_fusion
  (1 shorter events, 0.0 us)
Async XLA Ops:
  0.6 4.4 %copy-start.5 = (f32[128]{0:T(128)S(1)}, f32[128]{0:T(128)}, u32[]{:S(2)}) copy-start(f32[128]{0:T(128)} %param.15) | copy-start | bytes 1540
  0.6 4.4 %copy-start.4 = (s32[128]{0:T(128)S(1)}, s32[128]{0:T(128)}, u32[]{:S(2)}) copy-start(s32[128]{0:T(128)} %param.14) | copy-start | bytes 1540
  0.7 4.4 %copy-start.3 = (f32[16]{0:T(128)S(1)}, f32[16]{0:T(128)}, u32[]{:S(2)}) copy-start(f32[16]{0:T(128)} %grid_ref.1) | copy-start | bytes 196
  0.7 4.4 %copy-start.2 = (s32[16]{0:T(128)S(1)}, s32[16]{0:T(128)}, u32[]{:S(2)}) copy-start(s32[16]{0:T(128)} %index_ref.1) | copy-start | bytes 196
  0.7 4.4 %copy-start.1 = (f32[16,49]{1,0:T(8,128)S(1)}, f32[16,49]{1,0:T(8,128)}, u32[]{:S(2)}) copy-start(f32[16,49]{1,0:T(8,128)} %se_ref.1) | copy-start | bytes 9412
  0.7 4.4 %copy-start = (f32[49,8192]{1,0:T(8,128)S(1)}, f32[49,8192]{1,0:T(8,128)}, u32[]{:S(2)}) copy-start(f32[49,8192]{1,0:T(8,128)} %effects_hbm.1) | copy-start | bytes 4816900

commit v4 on v3

--- a/solution.py
+++ b/solution.py
@@ -3,6 +3,7 @@
 
 import jax
 import jax.numpy as jnp
+import numpy as np
 from jax import lax
 from jax.experimental import pallas as pl
 from jax.experimental.pallas import tpu as pltpu
@@ -12,6 +13,7 @@
 SUB = 8
 LANES = 128
 PIECES = 5
+GROUP = 5
 
 
 def block_edge(count):
@@ -22,16 +24,29 @@
     return pl.ds(pl.multiple_of(index * SUB, SUB), SUB)
 
 
-def eliminate(n, table, pivots, factors):
+def update_plan(blocks, group):
+    lists = []
+    for kb in range(blocks):
+        pairs = [(ib, jb) for ib in range(kb + 1, blocks) for jb in list(range(kb)) + list(range(ib + 1, blocks))]
+        while len(pairs) % group:
+            pairs.append((blocks, 0))
+        lists.append(pairs)
+    flat = [pair for pairs in lists for pair in pairs]
+    starts = np.cumsum([0] + [len(pairs) for pairs in lists])
+    ends = [starts[kb] + sum(ib < blocks for ib, _ in pairs) for kb, pairs in enumerate(lists)]
+    return tuple(np.array(a, np.int32) for a in ([p[0] for p in flat], [p[1] for p in flat], starts, ends))
+
+
+def elimination(n, table, pivots, factors):
     edge = block_edge(n)
     blocks = n // edge
 
-    def at(i, j):
-        return element(i * n + j)
-
-    def one_pivot_block(kb, carry):
+    def at(q, i, j):
+        return element(q * (n + edge) * n + i * n + j)
+
+    def pivot_stage(q, kb):
         first = kb * edge
-        diag = [[table[at(first + m, first + j), :] if j >= m else None for j in range(edge)] for m in range(edge)]
+        diag = [[table[at(q, first + m, first + j), :] if j >= m else None for j in range(edge)] for m in range(edge)]
         lower = [[None] * edge for _ in range(edge)]
         inverse = [[None] * edge for _ in range(edge)]
         recips = []
@@ -50,18 +65,18 @@
                 inverse[r][m] = -lower[r][m]
         for r in range(edge):
             for j in range(r):
-                table[at(first + r, first + j), :] = inverse[r][j]
+                table[at(q, first + r, first + j), :] = inverse[r][j]
 
         def column_block(jb, with_factor):
             col = jb * edge
             for j in range(edge):
-                rows = [table[at(first + m, col + j), :] for m in range(edge)]
+                rows = [table[at(q, first + m, col + j), :] for m in range(edge)]
                 for m in range(edge):
                     for r in range(m + 1, edge):
                         rows[r] = rows[r] - lower[r][m] * rows[m]
                 for m in range(edge):
                     if m:
-                        table[at(first + m, col + j), :] = rows[m]
+                        table[at(q, first + m, col + j), :] = rows[m]
                     if with_factor:
                         factors[element(m * n + col + j), :] = rows[m] * recips[m]
 
@@ -86,45 +101,40 @@
                 for j in range(edge):
                     totals = [f[a][j] for a in range(size)]
                     for m in range(j + 1, edge):
-                        v = table[at(first + m, first + j), :]
+                        v = table[at(q, first + m, first + j), :]
                         totals = [totals[a] + f[a][m] * v for a in range(size)]
                     for a, i in enumerate(rows):
-                        table[at(row + i, first + j), :] = -totals[a]
+                        table[at(q, row + i, first + j), :] = -totals[a]
                 for j in range(rows[0], edge):
                     live = [a for a, i in enumerate(rows) if i <= j]
-                    values = [table[at(row + rows[a], row + j), :] for a in live]
+                    values = [table[at(q, row + rows[a], row + j), :] for a in live]
                     for m in range(edge):
-                        u = table[at(first + m, row + j), :]
+                        u = table[at(q, first + m, row + j), :]
                         values = [v - f[a][m] * u for a, v in zip(live, values)]
                     for a, v in zip(live, values):
-                        table[at(row + rows[a], row + j), :] = v
-
-            def full(index, cc):
-                jb = jnp.where(index < kb, index, index - kb + ib + 1)
-                col = jb * edge
-                start = 0
-                for size in (edge - edge // 2, edge // 2):
-                    rows = range(start, start + size)
-                    start += size
-                    held = [[table[at(row + i, col + j), :] for j in range(edge)] for i in rows]
-                    for m in range(edge):
-                        f = [factors[element(m * n + row + i), :] for i in rows]
-                        for j in range(edge):
-                            u = table[at(first + m, col + j), :]
-                            for a in range(len(f)):
-                                held[a][j] = held[a][j] - f[a] * u
-                    for a, i in enumerate(rows):
-                        for j in range(edge):
-                            table[at(row + i, col + j), :] = held[a][j]
-                return cc
-
-            lax.fori_loop(0, kb + blocks - 1 - ib, full, 0)
+                        table[at(q, row + rows[a], row + j), :] = v
             return c
 
         lax.fori_loop(kb + 1, blocks, row_block, 0)
-        return carry
-
-    lax.fori_loop(0, blocks, one_pivot_block, 0)
+
+    def update(q, kb, ib, jb):
+        first, row, col = kb * edge, ib * edge, jb * edge
+        start = 0
+        for size in (edge - edge // 2, edge // 2):
+            rows = range(start, start + size)
+            start += size
+            held = [[table[at(q, row + i, col + j), :] for j in range(edge)] for i in rows]
+            for m in range(edge):
+                f = [factors[element(m * n + row + i), :] for i in rows]
+                for j in range(edge):
+                    u = table[at(q, first + m, col + j), :]
+                    for a in range(len(f)):
+                        held[a][j] = held[a][j] - f[a] * u
+            for a, i in enumerate(rows):
+                for j in range(edge):
+                    table[at(q, row + i, col + j), :] = held[a][j]
+
+    return at, pivot_stage, update
 
 
 def split3(value):
@@ -137,15 +147,17 @@
 
 def main_kernel(
     n, tiles, patterns, grids,
-    index_ref, grid_ref, effects_hbm, se_ref, covar_hbm, comp_grid_ref, prior_ref,
+    index_ref, grid_ref, plan_row, plan_col, plan_start, plan_end, effects_hbm, se_ref, covar_hbm, comp_grid_ref, prior_ref,
     out_hbm, peak_ref,
     table, pivots, factors, roots, halfdet, noise, weights, effects_ref, covar_ref, flipped, following, stack, acc, done, out_buf, se_rows,
     in_sem, covar_sem, out_sem,
-    count_s, start_s, slot_s, order_s,
+    count_s, start_s, slot_s, order_s, state_s,
 ):
     even = n // 16 * 16
     edge_rows = n - even
     edge = block_edge(n)
+    blocks = n // edge
+    at_block, pivot_stage, update = elimination(n, table, pivots, factors)
     fetch = pltpu.make_async_copy(effects_hbm, effects_ref, in_sem)
     fetch.start()
     fetch_covar = pltpu.make_async_copy(covar_hbm, covar_ref, covar_sem)
@@ -224,8 +236,9 @@
     def store(t, side):
         return pltpu.make_async_copy(out_buf.at[side], out_hbm.at[:, columns(t)], out_sem.at[side])
 
-    def one_batch(batch, carry):
+    def fill(batch):
         base = batch * SUB
+        q = lax.rem(batch, 2)
         for s in range(SUB):
             b = slot_s[jnp.minimum(base + s, used - 1)]
             se_rows[pl.ds(s, 1), :] = se_ref[pl.ds(b, 1), :]
@@ -234,17 +247,63 @@
         for i in range(n):
             noise[pl.ds(i * SUB, SUB), :] = jnp.broadcast_to(squares[:, i : i + 1], (SUB, LANES))
 
-        for rb in range(n // edge):
+        for rb in range(blocks):
             def fill_row(i, c):
                 for j in range(rb * edge, n):
-                    e = i * n + j
-                    table[element(e), :] = covar_ref[pl.ds(e, SUB, stride=0), :] * scale
-                d = element(i * n + i)
+                    table[at_block(q, i, j), :] = covar_ref[pl.ds(i * n + j, SUB, stride=0), :] * scale
+                d = at_block(q, i, i)
                 table[d, :] = table[d, :] + noise[element(i), :]
                 return c
 
             lax.fori_loop(rb * edge, (rb + 1) * edge, fill_row, 0)
-        eliminate(n, table, pivots, factors)
+
+    def advance(q):
+        kb = state_s[0]
+
+        @pl.when(state_s[1] >= plan_start[kb + 1])
+        def _():
+            state_s[0] = kb + 1
+
+            @pl.when(kb + 1 < blocks)
+            def _():
+                pivot_stage(q, kb + 1)
+
+    def begin(q):
+        state_s[0] = 0
+        state_s[1] = 0
+        pivot_stage(q, 0)
+
+    def drain(q):
+        def one_block(kb, c):
+            position = state_s[1]
+
+            def one(p, cc):
+                update(q, kb, plan_row[p], plan_col[p])
+                return cc
+
+            lax.fori_loop(position, plan_end[kb], one, 0)
+            state_s[1] = plan_start[kb + 1]
+
+            @pl.when(kb + 1 < blocks)
+            def _():
+                pivot_stage(q, kb + 1)
+
+            return c
+
+        lax.fori_loop(state_s[0], blocks, one_block, 0)
+
+    def one_batch(batch, carry):
+        base = batch * SUB
+        q = lax.rem(batch, 2)
+        more = base + SUB < used
+
+        @pl.when(batch == 0)
+        def _():
+            fill(batch)
+            begin(q)
+
+        drain(q)
+        state_s[0] = blocks
         logs = jnp.zeros((SUB, LANES), jnp.float32)
         for i in range(n):
             d = pivots[pl.ds(i * SUB, SUB), :]
@@ -257,13 +316,18 @@
             fetch.wait()
             prepare(order_s[0], following)
 
+        @pl.when(more)
+        def _():
+            fill(batch + 1)
+            begin(1 - q)
+
         def one_slot(slot, c):
             s = slot - base
             for i in range(n):
                 groups = min(i // 16 + 1, even // 16)
                 rows = groups * 16
                 root = roots[pl.ds(i * SUB + s, SUB, stride=0), :][0:1, :]
-                row = table[pl.ds(i * n * SUB + s, rows, stride=SUB), :]
+                row = table[pl.ds(q * (n + edge) * n * SUB + i * n * SUB + s, rows, stride=SUB), :]
                 if i < even:
                     j = lax.broadcasted_iota(jnp.int32, (rows, LANES), 0)
                     row = jnp.where(j < i, row, jnp.where(j == i, 1.0, 0.0))
@@ -290,23 +354,40 @@
                 def _():
                     store(0, 1 - side).wait()
 
-                flipped[...] = following[...]
-                prepare(order_s[place_at + 1], following)
-                conclude(before, 1 - side)
-                for i in range(0, n, 2):
-                    if i + 1 < n:
-                        right = jnp.concatenate([weights[i], weights[i + 1]], axis=1)
-                    else:
-                        right = weights[i]
-                    white = jnp.dot(flipped[...], right, preferred_element_type=jnp.float32)
-                    square = white[:, :LANES] * white[:, :LANES]
-                    if i + 1 < n:
-                        square = square + white[:, LANES:] * white[:, LANES:]
-                    if i:
-                        acc[...] += square
-                    else:
-                        acc[...] = square
-                done[...] = row_const - 0.5 * acc[...]
+                def body(beside):
+                    flipped[...] = following[...]
+                    prepare(order_s[place_at + 1], following)
+                    conclude(before, 1 - side)
+                    for i in range(0, n, 2):
+                        if i + 1 < n:
+                            right = jnp.concatenate([weights[i], weights[i + 1]], axis=1)
+                        else:
+                            right = weights[i]
+                        white = jnp.dot(flipped[...], right, preferred_element_type=jnp.float32)
+                        square = white[:, :LANES] * white[:, :LANES]
+                        if i + 1 < n:
+                            square = square + white[:, LANES:] * white[:, LANES:]
+                        if i:
+                            acc[...] += square
+                        else:
+                            acc[...] = square
+                        if beside is not None and i % 10 == 2 and i // 10 < GROUP:
+                            beside(i // 10)
+                    done[...] = row_const - 0.5 * acc[...]
+
+                kb = state_s[0]
+                position = state_s[1]
+                working = kb < blocks
+
+                @pl.when(working)
+                def _():
+                    body(lambda g: update(1 - q, kb, plan_row[position + g], plan_col[position + g]))
+                    state_s[1] = position + GROUP
+                    advance(1 - q)
+
+                @pl.when(jnp.logical_not(working))
+                def _():
+                    body(None)
 
                 @pl.when(place_at >= 1)
                 def _():
@@ -339,6 +420,8 @@
     even = n // 16 * 16
     assert covar.shape == (n * n, LANES) and (n - even) * PIECES <= 16
     depth = PIECES * even + 16
+    edge = block_edge(n)
+    plan = update_plan(n // edge, GROUP)
     vmem = pl.BlockSpec(memory_space=pltpu.VMEM)
     smem = pl.BlockSpec(memory_space=pltpu.SMEM)
     hbm = pl.BlockSpec(memory_space=pl.ANY)
@@ -350,12 +433,12 @@
             jax.ShapeDtypeStruct((LANES, pairs), f32),
             jax.ShapeDtypeStruct((2, pairs), f32),
         ),
-        in_specs=[smem, smem, hbm, vmem, hbm, vmem, vmem],
+        in_specs=[smem] * 6 + [hbm, vmem, hbm, vmem, vmem],
         out_specs=(hbm, vmem),
         scratch_shapes=[
-            pltpu.VMEM((n * n * SUB, LANES), f32),
+            pltpu.VMEM((2 * (n + edge) * n * SUB, LANES), f32),
             pltpu.VMEM((n * SUB, LANES), f32),
-            pltpu.VMEM((block_edge(n) * n * SUB, LANES), f32),
+            pltpu.VMEM(((edge * n + edge) * SUB, LANES), f32),
             pltpu.VMEM((n * SUB, LANES), f32),
             pltpu.VMEM((SUB, LANES), f32),
             pltpu.VMEM((n * SUB, LANES), f32),
@@ -376,9 +459,10 @@
             pltpu.SMEM((patterns + 1,), jnp.int32),
             pltpu.SMEM((patterns + 1,), jnp.int32),
             pltpu.SMEM((tiles + 1,), jnp.int32),
+            pltpu.SMEM((2,), jnp.int32),
         ],
-        compiler_params=pltpu.CompilerParams(vmem_limit_bytes=26 * 1024 * 1024),
-    )(se_index, grid_scale, effects, se_table, covar, comp_grid[None], weights[None])
+        compiler_params=pltpu.CompilerParams(vmem_limit_bytes=40 * 1024 * 1024),
+    )(se_index, grid_scale, *plan, effects, se_table, covar, comp_grid[None], weights[None])
 
 
 def exact_dot(left, right, dims):

time: 92.1 us -> 89.2 us (0.969)
  blocking collectives: 33.2 us -> 16.3 us
  Pallas kernels: 52.9 us -> 66.7 us
    all_to_all x1, blocking collectives: 31.2 us -> 14.3 us  [per_device(): masses = jnp.sum(lax.all_to_all(mass, 'pairs', 0, 0, tiled=True), axis=0)]
    pallas_call x1, Pallas kernels: 49.8 us -> 63.6 us  [shifted_scores(): pl.pallas_call(functools.partial(main_kernel, n, tiles, patterns, grid_sc...]
where the time goes in v4:
time: 89.2 us; the launch traced here: 88.8 us
  Pallas kernels  66.7 us (75%)
  blocking collectives  16.3 us (18%)
  matrix products  4.15 us (5%)
    pallas_call x1, Pallas kernels, shifted_scores(): pl.pallas_call(functools.partial(main_kernel, n, tiles, patterns, grid_sc...  63.6 us
    all_to_all x1, blocking collectives, per_device(): masses = jnp.sum(lax.all_to_all(mass, 'pairs', 0, 0, tiled=True), axis=0)  14.3 us
    pallas_call x1, Pallas kernels, finish(): pl.pallas_call(functools.partial(finish_kernel, width), name='finish', in...  3.12 us
    dot_general x1, matrix products, per_device(): jnp.einsum('uij,ukj->uik', base_root, base_root, precision=lax.Precision....  2.33 us
    all_gather x1, blocking collectives, per_device(): peaks = lax.all_gather(peak, 'comp')  2.04 us
    dot_general x1, matrix products, exact_dot(): lax.dot_general(left, right, (dims, ((), ())), precision=lax.Precision.HI...  1.82 us

profile of v4, /device:TPU:0, one launch (start us, length us, event | category | flops | bytes accessed | tf_op | source)
XLA Modules:
  0.0 88.8 jit_solution(3825993789764920964)
XLA Ops:
  0.6 0.0 copy-start.6
  0.6 0.0 copy-start.7
  0.7 0.0 copy-start.8
  0.7 0.0 copy-start.9
  0.7 0.0 copy-start.5
  0.7 0.0 copy-start.4
  0.7 0.0 copy-start.3
  0.7 0.0 copy-start.2
  0.7 0.0 copy-start.1
  0.7 0.0 copy-start
  0.7 2.3 %fusion = f32[16,49,49]{2,1,0:T(8,128)S(1)} fusion(f32[16,49,49]{2,0,1:T(8,128)} %param.15), kind=kOutput, calls=%fused_computation | convolution fusion | flops 22588608 | bytes 307328 | tf_op jit(solution)/shard_map/uij,ukj->uik/dot_general | solution.py:522
  3.1 0.2 reshape.12
  3.2 1.8 %fusion.2.covar_hbm = f32[2401,128]{1,0:T(8,128)S(1)} fusion(f32[16,2401]{1,0:T(8,128)S(1)} %reshape.12, s32[128]{0:T(128)} %param.17), kind=kOutput, calls=%fused_computation.3 | convolution fusion | flops 59009024 | bytes 1383488 | tf_op jit(solution)/shard_map/dot_general | solution.py:469
  5.1 0.0 copy-done.6
  5.1 0.0 copy-done.7
  5.1 0.0 copy-done.8
  5.1 0.0 copy-done.9
  5.1 0.0 copy-done.5
  5.1 0.0 copy-done.4
  5.2 63.6 %shifted_scores.1 = (f32[128,8192]{1,0:T(8,128)S(1)}, f32[2,8192]{1,0:T(2,128)S(1)}) custom-call(s32[16]{0:T(128)S(1)} %copy-done.2, f32[16]{0:T(128)S(1)} %copy-done.3, s32[75]{0:T(128)S(1)} %copy-done.9, s32[75]{0:T(128)S(1)} %copy-done.8, s32[8]{0:T(128)S(1)} %copy-done.7, s32[7]{0:T(128)S(1)} %copy-done.6, f32[49,8192]{1,0:T(8,128)S(1)} %copy-done, ...), custom_call_target="tpu_custom_call" | custom-call | tf_op jit(solution)/shard_map/shifted_scores/pallas_call | solution.py:429
  68.8 2.0 %all-gather.1.peaks_ref = f32[2,2,8192]{2,1,0:T(2,128)S(1)} all-gather(f32[1,2,8192]{2,1,0:T(2,128)S(1)} %bitcast.8), channel_id=2, replica_groups=mesh['pairs'=16,'comp'=2] {'comp'}, dimensions={0}, use_global_device_ids=true | all-gather | bytes 196608 | tf_op jit(solution)/shard_map/all_gather | solution.py:528
  70.8 3.1 %finish.1 = (f32[128,8192]{1,0:T(8,128)}, f32[1,8192]{1,0:T(1,128)}, f32[16,128]{1,0:T(8,128)S(1)}) custom-call(f32[128,8192]{1,0:T(8,128)S(1)} %get-tuple-element.8.shifted_ref, f32[2,8192]{1,0:T(2,128)S(1)} %get-tuple-element.9.own_ref, f32[2,2,8192]{2,1,0:T(2,128)S(1)} %all-gather.1.peaks_ref), custom_call_target="tpu_custom_call" | custom-call | tf_op jit(solution)/shard_map/finish/pallas_call | solution.py:504
  73.9 14.3 %all_to_all.9 = f32[16,1,128]{2,1,0:T(1,128)S(1)} all-to-all(f32[16,1,128]{2,1,0:T(1,128)S(1)} %bitcast.9), channel_id=1, replica_groups=mesh['pairs'=16,'comp'=2] {'pairs'}, dimensions={0} | all-to-all | bytes 16384 | tf_op jit(solution)/shard_map/all_to_all | solution.py:531
  88.2 0.5 multiply_log_fusion
  (5 shorter events, 0.0 us)
Async XLA Ops:
  0.6 4.4 %copy-start.6 = (s32[7]{0:T(128)S(1)}, s32[7]{0:T(128)}, u32[]{:S(2)}) copy-start(s32[7]{0:T(128)} %constant.18.clone.plan_end) | copy-start | bytes 88
  0.6 4.4 %copy-start.7 = (s32[8]{0:T(128)S(1)}, s32[8]{0:T(128)}, u32[]{:S(2)}) copy-start(s32[8]{0:T(128)} %constant.17.clone.plan_start) | copy-start | bytes 100
  0.7 4.4 %copy-start.8 = (s32[75]{0:T(128)S(1)}, s32[75]{0:T(128)}, u32[]{:S(2)}) copy-start(s32[75]{0:T(128)} %constant.16.clone.plan_col) | copy-start | bytes 904
  0.7 4.4 %copy-start.9 = (s32[75]{0:T(128)S(1)}, s32[75]{0:T(128)}, u32[]{:S(2)}) copy-start(s32[75]{0:T(128)} %constant.15.clone.plan_row) | copy-start | bytes 904
  0.7 4.4 %copy-start.5 = (f32[128]{0:T(128)S(1)}, f32[128]{0:T(128)}, u32[]{:S(2)}) copy-start(f32[128]{0:T(128)} %param.19) | copy-start | bytes 1540
  0.7 4.4 %copy-start.4 = (s32[128]{0:T(128)S(1)}, s32[128]{0:T(128)}, u32[]{:S(2)}) copy-start(s32[128]{0:T(128)} %param.18) | copy-start | bytes 1540
  0.7 4.4 %copy-start.3 = (f32[16]{0:T(128)S(1)}, f32[16]{0:T(128)}, u32[]{:S(2)}) copy-start(f32[16]{0:T(128)} %grid_ref.1) | copy-start | bytes 196
  0.7 4.4 %copy-start.2 = (s32[16]{0:T(128)S(1)}, s32[16]{0:T(128)}, u32[]{:S(2)}) copy-start(s32[16]{0:T(128)} %index_ref.1) | copy-start | bytes 196
  0.7 4.4 %copy-start.1 = (f32[16,49]{1,0:T(8,128)S(1)}, f32[16,49]{1,0:T(8,128)}, u32[]{:S(2)}) copy-start(f32[16,49]{1,0:T(8,128)} %se_ref.1) | copy-start | bytes 9412
  0.7 4.4 %copy-start = (f32[49,8192]{1,0:T(8,128)S(1)}, f32[49,8192]{1,0:T(8,128)}, u32[]{:S(2)}) copy-start(f32[49,8192]{1,0:T(8,128)} %effects_hbm.1) | copy-start | bytes 4816900

commit v5 on v4

--- a/solution.py
+++ b/solution.py
@@ -14,6 +14,7 @@
 LANES = 128
 PIECES = 5
 GROUP = 5
+ROWS = 3
 
 
 def block_edge(count):
@@ -93,26 +94,31 @@
 
         def row_block(ib, c):
             row = ib * edge
-            start = 0
-            for size in (edge - edge // 2, edge // 2):
-                rows = range(start, start + size)
-                start += size
+            for start in range(0, edge, ROWS):
+                rows = range(start, min(start + ROWS, edge))
+                size = len(rows)
                 f = [[factors[element(m * n + row + i), :] for m in range(edge)] for i in rows]
-                for j in range(edge):
-                    totals = [f[a][j] for a in range(size)]
-                    for m in range(j + 1, edge):
+                totals = [list(line) for line in f]
+                for m in range(1, edge):
+                    for j in range(m):
                         v = table[at(q, first + m, first + j), :]
-                        totals = [totals[a] + f[a][m] * v for a in range(size)]
-                    for a, i in enumerate(rows):
-                        table[at(q, row + i, first + j), :] = -totals[a]
+                        for a in range(size):
+                            totals[a][j] = totals[a][j] + f[a][m] * v
+                values = {}
                 for j in range(rows[0], edge):
                     live = [a for a, i in enumerate(rows) if i <= j]
-                    values = [table[at(q, row + rows[a], row + j), :] for a in live]
+                    for a in live:
+                        values[a, j] = table[at(q, row + rows[a], row + j), :]
                     for m in range(edge):
                         u = table[at(q, first + m, row + j), :]
-                        values = [v - f[a][m] * u for a, v in zip(live, values)]
-                    for a, v in zip(live, values):
-                        table[at(q, row + rows[a], row + j), :] = v
+                        for a in live:
+                            values[a, j] = values[a, j] - f[a][m] * u
+                for a, i in enumerate(rows):
+                    for j in range(edge):
+                        table[at(q, row + i, first + j), :] = -totals[a][j]
+                for (a, j), v in values.items():
+                    table[at(q, row + rows[a], row + j), :] = v
+
             return c
 
         lax.fori_loop(kb + 1, blocks, row_block, 0)

time: 89.2 us -> 86.6 us (0.971)
  Pallas kernels: 66.7 us -> 63 us
    pallas_call x1, Pallas kernels: 63.6 us -> 59.8 us  [shifted_scores(): pl.pallas_call(functools.partial(main_kernel, n, tiles, patterns, grid_sc...]
where the time goes in v5:
time: 86.6 us; the launch traced here: 85.8 us
  Pallas kernels  63 us (73%)
  blocking collectives  17.1 us (20%)
  matrix products  4.15 us (5%)
    pallas_call x1, Pallas kernels, shifted_scores(): pl.pallas_call(functools.partial(main_kernel, n, tiles, patterns, grid_sc...  59.8 us
    all_to_all x1, blocking collectives, per_device(): masses = jnp.sum(lax.all_to_all(mass, 'pairs', 0, 0, tiled=True), axis=0)  15.1 us
    pallas_call x1, Pallas kernels, finish(): pl.pallas_call(functools.partial(finish_kernel, width), name='finish', in...  3.12 us
    dot_general x1, matrix products, per_device(): jnp.einsum('uij,ukj->uik', base_root, base_root, precision=lax.Precision....  2.33 us
    all_gather x1, blocking collectives, per_device(): peaks = lax.all_gather(peak, 'comp')  2.04 us
    dot_general x1, matrix products, exact_dot(): lax.dot_general(left, right, (dims, ((), ())), precision=lax.Precision.HI...  1.82 us

profile of v5, /device:TPU:0, one launch (start us, length us, event | category | flops | bytes accessed | tf_op | source)
XLA Modules:
  0.0 85.8 jit_solution(7848024853912478423)
XLA Ops:
  0.6 0.0 copy-start.6
  0.6 0.0 copy-start.7
  0.7 0.0 copy-start.8
  0.7 0.0 copy-start.9
  0.7 0.0 copy-start.5
  0.7 0.0 copy-start.4
  0.7 0.0 copy-start.3
  0.7 0.0 copy-start.2
  0.7 0.0 copy-start.1
  0.7 0.0 copy-start
  0.7 2.3 %fusion = f32[16,49,49]{2,1,0:T(8,128)S(1)} fusion(f32[16,49,49]{2,0,1:T(8,128)} %param.15), kind=kOutput, calls=%fused_computation | convolution fusion | flops 22588608 | bytes 307328 | tf_op jit(solution)/shard_map/uij,ukj->uik/dot_general | solution.py:528
  3.1 0.2 reshape.12
  3.2 1.8 %fusion.2.covar_hbm = f32[2401,128]{1,0:T(8,128)S(1)} fusion(f32[16,2401]{1,0:T(8,128)S(1)} %reshape.12, s32[128]{0:T(128)} %param.17), kind=kOutput, calls=%fused_computation.3 | convolution fusion | flops 59009024 | bytes 1383488 | tf_op jit(solution)/shard_map/dot_general | solution.py:475
  5.1 0.0 copy-done.6
  5.1 0.0 copy-done.7
  5.1 0.0 copy-done.8
  5.1 0.0 copy-done.9
  5.1 0.0 copy-done.5
  5.1 0.0 copy-done.4
  5.2 59.8 %shifted_scores.1 = (f32[128,8192]{1,0:T(8,128)S(1)}, f32[2,8192]{1,0:T(2,128)S(1)}) custom-call(s32[16]{0:T(128)S(1)} %copy-done.2, f32[16]{0:T(128)S(1)} %copy-done.3, s32[75]{0:T(128)S(1)} %copy-done.9, s32[75]{0:T(128)S(1)} %copy-done.8, s32[8]{0:T(128)S(1)} %copy-done.7, s32[7]{0:T(128)S(1)} %copy-done.6, f32[49,8192]{1,0:T(8,128)S(1)} %copy-done, ...), custom_call_target="tpu_custom_call" | custom-call | tf_op jit(solution)/shard_map/shifted_scores/pallas_call | solution.py:435
  65.0 2.0 %all-gather.1.peaks_ref = f32[2,2,8192]{2,1,0:T(2,128)S(1)} all-gather(f32[1,2,8192]{2,1,0:T(2,128)S(1)} %bitcast.8), channel_id=2, replica_groups=mesh['pairs'=16,'comp'=2] {'comp'}, dimensions={0}, use_global_device_ids=true | all-gather | bytes 196608 | tf_op jit(solution)/shard_map/all_gather | solution.py:534
  67.1 3.1 %finish.1 = (f32[128,8192]{1,0:T(8,128)}, f32[1,8192]{1,0:T(1,128)}, f32[16,128]{1,0:T(8,128)S(1)}) custom-call(f32[128,8192]{1,0:T(8,128)S(1)} %get-tuple-element.8.shifted_ref, f32[2,8192]{1,0:T(2,128)S(1)} %get-tuple-element.9.own_ref, f32[2,2,8192]{2,1,0:T(2,128)S(1)} %all-gather.1.peaks_ref), custom_call_target="tpu_custom_call" | custom-call | tf_op jit(solution)/shard_map/finish/pallas_call | solution.py:510
  70.2 15.1 %all_to_all.9 = f32[16,1,128]{2,1,0:T(1,128)S(1)} all-to-all(f32[16,1,128]{2,1,0:T(1,128)S(1)} %bitcast.9), channel_id=1, replica_groups=mesh['pairs'=16,'comp'=2] {'pairs'}, dimensions={0} | all-to-all | bytes 16384 | tf_op jit(solution)/shard_map/all_to_all | solution.py:537
  85.3 0.5 multiply_log_fusion
  (5 shorter events, 0.0 us)
Async XLA Ops:
  0.6 4.4 %copy-start.6 = (s32[7]{0:T(128)S(1)}, s32[7]{0:T(128)}, u32[]{:S(2)}) copy-start(s32[7]{0:T(128)} %constant.18.clone.plan_end) | copy-start | bytes 88
  0.6 4.4 %copy-start.7 = (s32[8]{0:T(128)S(1)}, s32[8]{0:T(128)}, u32[]{:S(2)}) copy-start(s32[8]{0:T(128)} %constant.17.clone.plan_start) | copy-start | bytes 100
  0.7 4.4 %copy-start.8 = (s32[75]{0:T(128)S(1)}, s32[75]{0:T(128)}, u32[]{:S(2)}) copy-start(s32[75]{0:T(128)} %constant.16.clone.plan_col) | copy-start | bytes 904
  0.7 4.4 %copy-start.9 = (s32[75]{0:T(128)S(1)}, s32[75]{0:T(128)}, u32[]{:S(2)}) copy-start(s32[75]{0:T(128)} %constant.15.clone.plan_row) | copy-start | bytes 904
  0.7 4.4 %copy-start.5 = (f32[128]{0:T(128)S(1)}, f32[128]{0:T(128)}, u32[]{:S(2)}) copy-start(f32[128]{0:T(128)} %param.19) | copy-start | bytes 1540
  0.7 4.4 %copy-start.4 = (s32[128]{0:T(128)S(1)}, s32[128]{0:T(128)}, u32[]{:S(2)}) copy-start(s32[128]{0:T(128)} %param.18) | copy-start | bytes 1540
  0.7 4.4 %copy-start.3 = (f32[16]{0:T(128)S(1)}, f32[16]{0:T(128)}, u32[]{:S(2)}) copy-start(f32[16]{0:T(128)} %grid_ref.1) | copy-start | bytes 196
  0.7 4.4 %copy-start.2 = (s32[16]{0:T(128)S(1)}, s32[16]{0:T(128)}, u32[]{:S(2)}) copy-start(s32[16]{0:T(128)} %index_ref.1) | copy-start | bytes 196
  0.7 4.4 %copy-start.1 = (f32[16,49]{1,0:T(8,128)S(1)}, f32[16,49]{1,0:T(8,128)}, u32[]{:S(2)}) copy-start(f32[16,49]{1,0:T(8,128)} %se_ref.1) | copy-start | bytes 9412
  0.7 4.4 %copy-start = (f32[49,8192]{1,0:T(8,128)S(1)}, f32[49,8192]{1,0:T(8,128)}, u32[]{:S(2)}) copy-start(f32[49,8192]{1,0:T(8,128)} %effects_hbm.1) | copy-start | bytes 4816900

commit v6 on v5

--- a/solution.py
+++ b/solution.py
@@ -15,6 +15,8 @@
 PIECES = 5
 GROUP = 5
 ROWS = 3
+HEAD = 15
+SPAN = 16
 
 
 def block_edge(count):
@@ -34,8 +36,7 @@
         lists.append(pairs)
     flat = [pair for pairs in lists for pair in pairs]
     starts = np.cumsum([0] + [len(pairs) for pairs in lists])
-    ends = [starts[kb] + sum(ib < blocks for ib, _ in pairs) for kb, pairs in enumerate(lists)]
-    return tuple(np.array(a, np.int32) for a in ([p[0] for p in flat], [p[1] for p in flat], starts, ends))
+    return tuple(np.array(a, np.int32) for a in ([p[0] for p in flat], [p[1] for p in flat], starts))
 
 
 def elimination(n, table, pivots, factors):
@@ -153,9 +154,10 @@
 
 def main_kernel(
     n, tiles, patterns, grids,
-    index_ref, grid_ref, plan_row, plan_col, plan_start, plan_end, effects_hbm, se_ref, covar_hbm, comp_grid_ref, prior_ref,
+    index_ref, grid_ref, plan_row, plan_col, plan_start, effects_hbm, se_ref, covar_hbm, comp_grid_ref, prior_ref,
     out_hbm, peak_ref,
     table, pivots, factors, roots, halfdet, noise, weights, effects_ref, covar_ref, flipped, following, stack, acc, done, out_buf, se_rows,
+    scaled, forms, form_weights, doubled, products, features,
     in_sem, covar_sem, out_sem,
     count_s, start_s, slot_s, order_s, state_s,
 ):
@@ -205,6 +207,8 @@
 
     weights[...] = jnp.zeros_like(weights)
     stack[...] = jnp.zeros_like(stack)
+    forms[...] = jnp.zeros_like(forms)
+    doubled[...] = jnp.zeros_like(doubled)
     chosen = comp_grid_ref[...]
     scale = jnp.zeros(chosen.shape, jnp.float32)
     for g in range(grids):
@@ -216,6 +220,45 @@
 
     def columns(t):
         return pl.ds(pl.multiple_of(t * TILE, TILE), TILE)
+
+    def head_forms(q):
+        def line(i, a):
+            return pl.ds((i * HEAD + a) * SUB, SUB)
+
+        for i in range(HEAD):
+            root = roots[pl.ds(i * SUB, SUB), :]
+            for a in range(i):
+                scaled[line(i, a), :] = table[at_block(q, i, a), :] * root
+            scaled[line(i, i), :] = root
+        for a in range(HEAD):
+            own = {i: scaled[line(i, a), :] for i in range(a, HEAD)}
+            for b in range(a + 1):
+                total = None
+                for i in range(a, HEAD):
+                    term = own[i] * scaled[line(i, b), :]
+                    total = term if total is None else total + term
+                gap = a - b
+                d, j = (gap, b) if gap <= HEAD // 2 else (HEAD - gap, a)
+                forms[pl.ds((d * SPAN + j) * SUB, SUB), :] = total if gap == 0 else 2.0 * total
+
+    def head_features(t):
+        at = columns(t)
+        x = effects_ref[pl.ds(0, SPAN), at]
+        doubled[pl.ds(0, SPAN), :] = x
+        doubled[pl.ds(HEAD, SPAN), :] = x
+        j = lax.broadcasted_iota(jnp.int32, x.shape, 0)
+        x = jnp.where(j < HEAD, x, 0.0)
+        for d in range(LANES // SPAN):
+            products[pl.ds(d * SPAN, SPAN), :] = x * doubled[pl.ds(d, SPAN), :]
+        for piece, part in enumerate(split3(jnp.transpose(products[...]))):
+            features[:, piece * LANES : (piece + 1) * LANES] = part
+
+    def head_norm():
+        f = [features[:, p * LANES : (p + 1) * LANES] for p in range(3)]
+        w = [form_weights[pl.ds(p * LANES, LANES), :] for p in range(3)]
+        left = jnp.concatenate([f[0], f[0], f[1], f[1], f[0], f[2]], axis=1)
+        right = jnp.concatenate([w[0], w[1], w[0], w[1], w[2], w[0]], axis=0)
+        return jnp.dot(left, right, preferred_element_type=jnp.float32)
 
     def prepare(t, target):
         at = columns(t)
@@ -283,11 +326,12 @@
         def one_block(kb, c):
             position = state_s[1]
 
-            def one(p, cc):
-                update(q, kb, plan_row[p], plan_col[p])
+            def some(p, cc):
+                for g in range(GROUP):
+                    update(q, kb, plan_row[position + p * GROUP + g], plan_col[position + p * GROUP + g])
                 return cc
 
-            lax.fori_loop(position, plan_end[kb], one, 0)
+            lax.fori_loop(0, (plan_start[kb + 1] - position) // GROUP, some, 0)
             state_s[1] = plan_start[kb + 1]
 
             @pl.when(kb + 1 < blocks)
@@ -316,6 +360,7 @@
             roots[pl.ds(i * SUB, SUB), :] = lax.rsqrt(d)
             logs = logs + jnp.log(d)
         halfdet[...] = log_prior - 0.5 * logs
+        head_forms(q)
 
         @pl.when(batch == 0)
         def _():
@@ -329,7 +374,9 @@
 
         def one_slot(slot, c):
             s = slot - base
-            for i in range(n):
+            for piece, part in enumerate(split3(forms[pl.ds(s, LANES, stride=SUB), :])):
+                form_weights[pl.ds(piece * LANES, LANES), :] = part
+            for i in range(HEAD, n):
                 groups = min(i // 16 + 1, even // 16)
                 rows = groups * 16
                 root = roots[pl.ds(i * SUB + s, SUB, stride=0), :][0:1, :]
@@ -340,8 +387,8 @@
                 row = row * root
                 one = row.astype(jnp.bfloat16)
                 two = (row - one.astype(jnp.float32)).astype(jnp.bfloat16)
-                for piece, part in enumerate((one, one, two, two, one)):
-                    weights[i, pl.ds(piece * even, rows), :] = part
+                weights[i, pl.ds(0, rows), :] = one
+                weights[i, pl.ds(even, rows), :] = two
                 if i >= even:
                     first = root.astype(jnp.bfloat16)
                     second = (root - first.astype(jnp.float32)).astype(jnp.bfloat16)
@@ -349,8 +396,13 @@
                     tail = jnp.zeros((16, LANES), jnp.float32)
                     for piece, part in enumerate((first, first, second, second, first)):
                         tail = jnp.where(j == piece, part.astype(jnp.float32), tail)
-                    weights[i, pl.ds(PIECES * even, 16), :] = tail.astype(jnp.bfloat16)
+                    weights[i, pl.ds(2 * even, 16), :] = tail.astype(jnp.bfloat16)
             row_const = halfdet[pl.ds(s, 1), :]
+
+            def operand(i):
+                one = weights[i, pl.ds(0, even), :]
+                two = weights[i, pl.ds(even, even), :]
+                return jnp.concatenate([one, one, two, two, one, weights[i, pl.ds(2 * even, 16), :]], axis=0)
 
             def one_tile(place_at, cc):
                 before = order_s[jnp.maximum(place_at - 1, 0)]
@@ -364,22 +416,22 @@
                     flipped[...] = following[...]
                     prepare(order_s[place_at + 1], following)
                     conclude(before, 1 - side)
-                    for i in range(0, n, 2):
-                        if i + 1 < n:
-                            right = jnp.concatenate([weights[i], weights[i + 1]], axis=1)
-                        else:
-                            right = weights[i]
+                    head_features(order_s[place_at])
+                    for i in range(HEAD, n, 2):
+                        right = jnp.concatenate([operand(r) for r in range(i, min(i + 2, n))], axis=1)
                         white = jnp.dot(flipped[...], right, preferred_element_type=jnp.float32)
                         square = white[:, :LANES] * white[:, :LANES]
                         if i + 1 < n:
                             square = square + white[:, LANES:] * white[:, LANES:]
-                        if i:
+                        if i > HEAD:
                             acc[...] += square
                         else:
                             acc[...] = square
-                        if beside is not None and i % 10 == 2 and i // 10 < GROUP:
-                            beside(i // 10)
-                    done[...] = row_const - 0.5 * acc[...]
+                        if beside is not None:
+                            for g in range(GROUP):
+                                if (2 * g + 1) * (n - HEAD) // (2 * GROUP) // 2 == (i - HEAD) // 2:
+                                    beside(g)
+                    done[...] = row_const - 0.5 * (acc[...] + head_norm())
 
                 kb = state_s[0]
                 position = state_s[1]
@@ -439,7 +491,7 @@
             jax.ShapeDtypeStruct((LANES, pairs), f32),
             jax.ShapeDtypeStruct((2, pairs), f32),
         ),
-        in_specs=[smem] * 6 + [hbm, vmem, hbm, vmem, vmem],
+        in_specs=[smem] * 5 + [hbm, vmem, hbm, vmem, vmem],
         out_specs=(hbm, vmem),
         scratch_shapes=[
             pltpu.VMEM((2 * (n + edge) * n * SUB, LANES), f32),
@@ -448,7 +500,7 @@
             pltpu.VMEM((n * SUB, LANES), f32),
             pltpu.VMEM((SUB, LANES), f32),
             pltpu.VMEM((n * SUB, LANES), f32),
-            pltpu.VMEM((n, depth, LANES), jnp.bfloat16),
+            pltpu.VMEM((n, 2 * even + 16, LANES), jnp.bfloat16),
             pltpu.VMEM((n, pairs), f32),
             pltpu.VMEM((n * n, LANES), f32),
             pltpu.VMEM((TILE, depth), jnp.bfloat16),
@@ -458,6 +510,12 @@
             pltpu.VMEM((TILE, LANES), f32),
             pltpu.VMEM((2, LANES, TILE), f32),
             pltpu.VMEM((SUB, n), f32),
+            pltpu.VMEM((HEAD * HEAD * SUB, LANES), f32),
+            pltpu.VMEM((LANES * SUB, LANES), f32),
+            pltpu.VMEM((3 * LANES, LANES), jnp.bfloat16),
+            pltpu.VMEM((2 * SPAN, TILE), f32),
+            pltpu.VMEM((LANES, TILE), f32),
+            pltpu.VMEM((TILE, 3 * LANES), jnp.bfloat16),
             pltpu.SemaphoreType.DMA,
             pltpu.SemaphoreType.DMA,
             pltpu.SemaphoreType.DMA((2,)),

time: 86.6 us -> 83.1 us (0.960); the launches traced: 85.8 us -> 83.4 us
  Pallas kernels: 63 us -> 60.3 us
    pallas_call x1, Pallas kernels: 59.8 us -> 57.2 us  [shifted_scores(): pl.pallas_call(functools.partial(main_kernel, n, tiles, patterns, grid_sc...]
where the time goes in v6:
time: 83.1 us; the launch traced here: 83.4 us
  Pallas kernels  60.3 us (73%)
  blocking collectives  17.4 us (21%)
  matrix products  4.15 us (5%)
    pallas_call x1, Pallas kernels, shifted_scores(): pl.pallas_call(functools.partial(main_kernel, n, tiles, patterns, grid_sc...  57.2 us
    all_to_all x1, blocking collectives, per_device(): masses = jnp.sum(lax.all_to_all(mass, 'pairs', 0, 0, tiled=True), axis=0)  15.4 us
    pallas_call x1, Pallas kernels, finish(): pl.pallas_call(functools.partial(finish_kernel, width), name='finish', in...  3.13 us
    dot_general x1, matrix products, per_device(): jnp.einsum('uij,ukj->uik', base_root, base_root, precision=lax.Precision....  2.33 us
    all_gather x1, blocking collectives, per_device(): peaks = lax.all_gather(peak, 'comp')  2.02 us
    dot_general x1, matrix products, exact_dot(): lax.dot_general(left, right, (dims, ((), ())), precision=lax.Precision.HI...  1.82 us

profile of v6, /device:TPU:0, one launch (start us, length us, event | category | flops | bytes accessed | tf_op | source)
XLA Modules:
  0.0 83.4 jit_solution(563129611697352233)
XLA Ops:
  0.6 0.0 copy-start.6
  0.6 0.0 copy-start.7
  0.7 0.0 copy-start.8
  0.7 0.0 copy-start.5
  0.7 0.0 copy-start.4
  0.7 0.0 copy-start.3
  0.7 0.0 copy-start.2
  0.7 0.0 copy-start.1
  0.7 0.0 copy-start
  0.7 2.3 %fusion = f32[16,49,49]{2,1,0:T(8,128)S(1)} fusion(f32[16,49,49]{2,0,1:T(8,128)} %param.14), kind=kOutput, calls=%fused_computation | convolution fusion | flops 22588608 | bytes 307328 | tf_op jit(solution)/shard_map/uij,ukj->uik/dot_general | solution.py:586
  3.1 0.2 reshape.12
  3.2 1.8 %fusion.2.covar_hbm = f32[2401,128]{1,0:T(8,128)S(1)} fusion(f32[16,2401]{1,0:T(8,128)S(1)} %reshape.12, s32[128]{0:T(128)} %param.16), kind=kOutput, calls=%fused_computation.3 | convolution fusion | flops 59009024 | bytes 1383488 | tf_op jit(solution)/shard_map/dot_general | solution.py:533
  5.1 0.0 copy-done.6
  5.1 0.0 copy-done.7
  5.1 0.0 copy-done.8
  5.1 0.0 copy-done.5
  5.1 0.0 copy-done.4
  5.1 0.0 copy-done.3
  5.1 0.0 copy-done.2
  5.2 57.2 %shifted_scores.1 = (f32[128,8192]{1,0:T(8,128)S(1)}, f32[2,8192]{1,0:T(2,128)S(1)}) custom-call(s32[16]{0:T(128)S(1)} %copy-done.2, f32[16]{0:T(128)S(1)} %copy-done.3, s32[75]{0:T(128)S(1)} %copy-done.8, s32[75]{0:T(128)S(1)} %copy-done.7, s32[8]{0:T(128)S(1)} %copy-done.6, f32[49,8192]{1,0:T(8,128)S(1)} %copy-done, f32[16,49]{1,0:T(8,128)S(1)} %copy-done.1, ...), custom_call_target="tpu_custom_call" | custom-call | tf_op jit(solution)/shard_map/shifted_scores/pallas_call | solution.py:487
  62.3 2.0 %all-gather.1.peaks_ref = f32[2,2,8192]{2,1,0:T(2,128)S(1)} all-gather(f32[1,2,8192]{2,1,0:T(2,128)S(1)} %bitcast.8), channel_id=2, replica_groups=mesh['pairs'=16,'comp'=2] {'comp'}, dimensions={0}, use_global_device_ids=true | all-gather | bytes 196608 | tf_op jit(solution)/shard_map/all_gather | solution.py:592
  64.4 3.1 %finish.1 = (f32[128,8192]{1,0:T(8,128)}, f32[1,8192]{1,0:T(1,128)}, f32[16,128]{1,0:T(8,128)S(1)}) custom-call(f32[128,8192]{1,0:T(8,128)S(1)} %get-tuple-element.8.shifted_ref, f32[2,8192]{1,0:T(2,128)S(1)} %get-tuple-element.9.own_ref, f32[2,2,8192]{2,1,0:T(2,128)S(1)} %all-gather.1.peaks_ref), custom_call_target="tpu_custom_call" | custom-call | tf_op jit(solution)/shard_map/finish/pallas_call | solution.py:568
  67.5 15.4 %all_to_all.9 = f32[16,1,128]{2,1,0:T(1,128)S(1)} all-to-all(f32[16,1,128]{2,1,0:T(1,128)S(1)} %bitcast.9), channel_id=1, replica_groups=mesh['pairs'=16,'comp'=2] {'pairs'}, dimensions={0} | all-to-all | bytes 16384 | tf_op jit(solution)/shard_map/all_to_all | solution.py:595
  82.9 0.5 multiply_log_fusion
  (3 shorter events, 0.0 us)
Async XLA Ops:
  0.6 4.4 %copy-start.6 = (s32[8]{0:T(128)S(1)}, s32[8]{0:T(128)}, u32[]{:S(2)}) copy-start(s32[8]{0:T(128)} %constant.15.clone.plan_start) | copy-start | bytes 100
  0.6 4.4 %copy-start.7 = (s32[75]{0:T(128)S(1)}, s32[75]{0:T(128)}, u32[]{:S(2)}) copy-start(s32[75]{0:T(128)} %constant.14.clone.plan_col) | copy-start | bytes 904
  0.7 4.4 %copy-start.8 = (s32[75]{0:T(128)S(1)}, s32[75]{0:T(128)}, u32[]{:S(2)}) copy-start(s32[75]{0:T(128)} %constant.13.clone.plan_row) | copy-start | bytes 904
  0.7 4.4 %copy-start.5 = (f32[128]{0:T(128)S(1)}, f32[128]{0:T(128)}, u32[]{:S(2)}) copy-start(f32[128]{0:T(128)} %param.18) | copy-start | bytes 1540
  0.7 4.4 %copy-start.4 = (s32[128]{0:T(128)S(1)}, s32[128]{0:T(128)}, u32[]{:S(2)}) copy-start(s32[128]{0:T(128)} %param.17) | copy-start | bytes 1540
  0.7 4.4 %copy-start.3 = (f32[16]{0:T(128)S(1)}, f32[16]{0:T(128)}, u32[]{:S(2)}) copy-start(f32[16]{0:T(128)} %grid_ref.1) | copy-start | bytes 196
  0.7 4.4 %copy-start.2 = (s32[16]{0:T(128)S(1)}, s32[16]{0:T(128)}, u32[]{:S(2)}) copy-start(s32[16]{0:T(128)} %index_ref.1) | copy-start | bytes 196
  0.7 4.4 %copy-start.1 = (f32[16,49]{1,0:T(8,128)S(1)}, f32[16,49]{1,0:T(8,128)}, u32[]{:S(2)}) copy-start(f32[16,49]{1,0:T(8,128)} %se_ref.1) | copy-start | bytes 9412
  0.7 4.4 %copy-start = (f32[49,8192]{1,0:T(8,128)S(1)}, f32[49,8192]{1,0:T(8,128)}, u32[]{:S(2)}) copy-start(f32[49,8192]{1,0:T(8,128)} %effects_hbm.1) | copy-start | bytes 4816900

commit v7 on v6

--- a/solution.py
+++ b/solution.py
@@ -154,11 +154,11 @@
 
 def main_kernel(
     n, tiles, patterns, grids,
-    index_ref, grid_ref, plan_row, plan_col, plan_start, effects_hbm, se_ref, covar_hbm, comp_grid_ref, prior_ref,
+    index_ref, grid_ref, plan_row, plan_col, plan_start, effects_hbm, se_ref, root_ref, comp_base_ref, comp_grid_ref, prior_ref,
     out_hbm, peak_ref,
-    table, pivots, factors, roots, halfdet, noise, weights, effects_ref, covar_ref, flipped, following, stack, acc, done, out_buf, se_rows,
+    table, pivots, factors, roots, halfdet, noise, weights, effects_ref, base_covar, covar_ref, flipped, following, stack, acc, done, out_buf, se_rows,
     scaled, forms, form_weights, doubled, products, features,
-    in_sem, covar_sem, out_sem,
+    in_sem, out_sem,
     count_s, start_s, slot_s, order_s, state_s,
 ):
     even = n // 16 * 16
@@ -168,8 +168,6 @@
     at_block, pivot_stage, update = elimination(n, table, pivots, factors)
     fetch = pltpu.make_async_copy(effects_hbm, effects_ref, in_sem)
     fetch.start()
-    fetch_covar = pltpu.make_async_copy(covar_hbm, covar_ref, covar_sem)
-    fetch_covar.start()
 
     def clear(b, c):
         count_s[b] = 0
@@ -216,7 +214,20 @@
     scale = jnp.broadcast_to(scale * scale, (SUB, LANES))
     log_prior = jnp.log(prior_ref[...]) - 0.5 * n * math.log(2.0 * math.pi)
 
-    fetch_covar.wait()
+    bases = root_ref.shape[0]
+    rows_up = (n + SUB - 1) // SUB * SUB
+    for u in range(bases):
+        root = root_ref[u]
+        base_covar[pl.ds(u * rows_up, n), 0:n] = lax.dot_general(
+            root, root, (((1,), (1,)), ((), ())), precision=lax.Precision.HIGHEST, preferred_element_type=jnp.float32
+        )
+    pick = lax.broadcasted_iota(jnp.int32, (bases, LANES), 0) == comp_base_ref[...]
+    pick = jnp.where(pick, 1.0, 0.0).astype(jnp.bfloat16)
+    pick = jnp.concatenate([pick, pick, pick], axis=0)
+    for i in range(n):
+        lines = jnp.concatenate(split3(base_covar[pl.ds(i, bases, stride=rows_up), :]), axis=0)
+        picked = lax.dot_general(lines, pick, (((0,), (0,)), ((), ())), preferred_element_type=jnp.float32)
+        covar_ref[pl.ds(i * rows_up, rows_up), :] = picked[:rows_up]
 
     def columns(t):
         return pl.ds(pl.multiple_of(t * TILE, TILE), TILE)
@@ -250,14 +261,14 @@
         x = jnp.where(j < HEAD, x, 0.0)
         for d in range(LANES // SPAN):
             products[pl.ds(d * SPAN, SPAN), :] = x * doubled[pl.ds(d, SPAN), :]
-        for piece, part in enumerate(split3(jnp.transpose(products[...]))):
+        for piece, part in enumerate(split3(jnp.transpose(products[...]))[:2]):
             features[:, piece * LANES : (piece + 1) * LANES] = part
 
     def head_norm():
-        f = [features[:, p * LANES : (p + 1) * LANES] for p in range(3)]
-        w = [form_weights[pl.ds(p * LANES, LANES), :] for p in range(3)]
-        left = jnp.concatenate([f[0], f[0], f[1], f[1], f[0], f[2]], axis=1)
-        right = jnp.concatenate([w[0], w[1], w[0], w[1], w[2], w[0]], axis=0)
+        f = [features[:, p * LANES : (p + 1) * LANES] for p in range(2)]
+        w = [form_weights[pl.ds(p * LANES, LANES), :] for p in range(2)]
+        left = jnp.concatenate([f[0], f[0], f[1], f[1]], axis=1)
+        right = jnp.concatenate([w[0], w[1], w[0], w[1]], axis=0)
         return jnp.dot(left, right, preferred_element_type=jnp.float32)
 
     def prepare(t, target):
@@ -299,7 +310,7 @@
         for rb in range(blocks):
             def fill_row(i, c):
                 for j in range(rb * edge, n):
-                    table[at_block(q, i, j), :] = covar_ref[pl.ds(i * n + j, SUB, stride=0), :] * scale
+                    table[at_block(q, i, j), :] = covar_ref[pl.ds(i * rows_up + j, SUB, stride=0), :] * scale
                 d = at_block(q, i, i)
                 table[d, :] = table[d, :] + noise[element(i), :]
                 return c
@@ -374,7 +385,7 @@
 
         def one_slot(slot, c):
             s = slot - base
-            for piece, part in enumerate(split3(forms[pl.ds(s, LANES, stride=SUB), :])):
+            for piece, part in enumerate(split3(forms[pl.ds(s, LANES, stride=SUB), :])[:2]):
                 form_weights[pl.ds(piece * LANES, LANES), :] = part
             for i in range(HEAD, n):
                 groups = min(i // 16 + 1, even // 16)
@@ -471,12 +482,14 @@
     store(last, side).wait()
 
 
-def shifted_scores(effects, se_table, se_index, covar, grid_scale, comp_grid, weights):
+def shifted_scores(effects, se_table, se_index, base_root, grid_scale, comp_base, comp_grid, weights):
     n, pairs = effects.shape
     patterns = se_table.shape[0]
     tiles = pairs // TILE
     even = n // 16 * 16
-    assert covar.shape == (n * n, LANES) and (n - even) * PIECES <= 16
+    bases = base_root.shape[0]
+    rows_up = (n + SUB - 1) // SUB * SUB
+    assert comp_grid.shape == (LANES,) and (n - even) * PIECES <= 16
     depth = PIECES * even + 16
     edge = block_edge(n)
     plan = update_plan(n // edge, GROUP)
@@ -491,7 +504,7 @@
             jax.ShapeDtypeStruct((LANES, pairs), f32),
             jax.ShapeDtypeStruct((2, pairs), f32),
         ),
-        in_specs=[smem] * 5 + [hbm, vmem, hbm, vmem, vmem],
+        in_specs=[smem] * 5 + [hbm, vmem, vmem, vmem, vmem, vmem],
         out_specs=(hbm, vmem),
         scratch_shapes=[
             pltpu.VMEM((2 * (n + edge) * n * SUB, LANES), f32),
@@ -502,7 +515,8 @@
             pltpu.VMEM((n * SUB, LANES), f32),
             pltpu.VMEM((n, 2 * even + 16, LANES), jnp.bfloat16),
             pltpu.VMEM((n, pairs), f32),
-            pltpu.VMEM((n * n, LANES), f32),
+            pltpu.VMEM((bases * rows_up, LANES), f32),
+            pltpu.VMEM((n * rows_up, LANES), f32),
             pltpu.VMEM((TILE, depth), jnp.bfloat16),
             pltpu.VMEM((TILE, depth), jnp.bfloat16),
             pltpu.VMEM((depth, TILE), f32),
@@ -512,11 +526,10 @@
             pltpu.VMEM((SUB, n), f32),
             pltpu.VMEM((HEAD * HEAD * SUB, LANES), f32),
             pltpu.VMEM((LANES * SUB, LANES), f32),
-            pltpu.VMEM((3 * LANES, LANES), jnp.bfloat16),
+            pltpu.VMEM((2 * LANES, LANES), jnp.bfloat16),
             pltpu.VMEM((2 * SPAN, TILE), f32),
             pltpu.VMEM((LANES, TILE), f32),
-            pltpu.VMEM((TILE, 3 * LANES), jnp.bfloat16),
-            pltpu.SemaphoreType.DMA,
+            pltpu.VMEM((TILE, 2 * LANES), jnp.bfloat16),
             pltpu.SemaphoreType.DMA,
             pltpu.SemaphoreType.DMA((2,)),
             pltpu.SMEM((patterns + 1,), jnp.int32),
@@ -526,11 +539,7 @@
             pltpu.SMEM((2,), jnp.int32),
         ],
         compiler_params=pltpu.CompilerParams(vmem_limit_bytes=40 * 1024 * 1024),
-    )(se_index, grid_scale, *plan, effects, se_table, covar, comp_grid[None], weights[None])
-
-
-def exact_dot(left, right, dims):
-    return lax.dot_general(left, right, (dims, ((), ())), precision=lax.Precision.HIGHEST, preferred_element_type=jnp.float32)
+    )(se_index, grid_scale, *plan, effects, se_table, base_root, comp_base[None], comp_grid[None], weights[None])
 
 
 def finish_kernel(width, shifted_ref, own_ref, peaks_ref, out_hbm, loglik_ref, mass_ref, buffer, sems):
@@ -583,12 +592,7 @@
 def per_device(effects, se_table, se_index, base_root, grid_scale, comp_base, comp_grid, weights):
     n, pairs = effects.shape
     comps = comp_base.shape[0]
-    covariances = jnp.einsum("uij,ukj->uik", base_root, base_root, precision=lax.Precision.HIGHEST)
-    covariances = covariances.reshape(covariances.shape[0], n * n)
-    bases = jnp.arange(covariances.shape[0], dtype=jnp.int32)
-    pick = (comp_base[None] == bases[:, None]).astype(jnp.float32)
-    covar = exact_dot(covariances, pick, ((0,), (0,)))
-    shifted, peak = shifted_scores(effects, se_table, se_index, covar, grid_scale, comp_grid, weights)
+    shifted, peak = shifted_scores(effects, se_table, se_index, base_root, grid_scale, comp_base, comp_grid, weights)
     peaks = lax.all_gather(peak, "comp")
     receivers = lax.axis_size("pairs")
     responsibility, loglik, mass = finish(shifted, peak, peaks, receivers)

time: 83.1 us -> 87.2 us (1.049); the launches traced: 83.4 us -> 85.6 us
  local copies, waits for them, and re-layouts: 0.21 us -> 8.56 us
  matrix products: 4.15 us -> 0 us
  blocking collectives: 17.4 us -> 15.8 us
    unnamed x18 -> x21, local copies, waits for them, and re-layouts: 0.05 us -> 8.56 us
    dot_general x2 -> x0, matrix products: 4.15 us -> none  [the longest x1 2.33 us: per_device(): jnp.einsum('uij,ukj->uik', base_root, base_root, precision=lax.Precision....]
    all_to_all x1, blocking collectives: 15.4 us -> 13.8 us  [per_device(): masses = jnp.sum(lax.all_to_all(mass, 'pairs', 0, 0, tiled=True), axis=0)]
where the time goes in v7:
time: 87.2 us; the launch traced here: 85.6 us
  Pallas kernels  60 us (69%)
  blocking collectives  15.8 us (18%)
  local copies, waits for them, and re-layouts  8.56 us (10%)
    pallas_call x1, Pallas kernels, shifted_scores(): pl.pallas_call(functools.partial(main_kernel, n, tiles, patterns, grid_sc...  56.9 us
    all_to_all x1, blocking collectives, per_device(): masses = jnp.sum(lax.all_to_all(mass, 'pairs', 0, 0, tiled=True), axis=0)  13.8 us
    unnamed x21, local copies, waits for them, and re-layouts  8.56 us
    pallas_call x1, Pallas kernels, finish(): pl.pallas_call(functools.partial(finish_kernel, width), name='finish', in...  3.13 us
    all_gather x1, blocking collectives, per_device(): peaks = lax.all_gather(peak, 'comp')  2.04 us

profile of v7, /device:TPU:0, one launch (start us, length us, event | category | flops | bytes accessed | tf_op | source)
XLA Modules:
  0.0 85.6 jit_solution(16003694280548110099)
XLA Ops:
  0.6 1.1 %copy.15.root_ref = f32[16,49,49]{2,1,0:T(8,128)S(1)} copy(f32[16,49,49]{2,0,1:T(8,128)} %param.14) | data formatting | bytes 307328 | tf_op args[3]
  1.8 0.0 copy-start
  1.8 1.5 %copy-done = f32[49,8192]{1,0:T(8,128)S(1)} copy-done((f32[49,8192]{1,0:T(8,128)S(1)}, f32[49,8192]{1,0:T(8,128)}, u32[]{:S(2)}) %copy-start) | copy-done | bytes 1605656
  3.3 0.0 copy-start.1
  3.3 0.7 copy-done.1
  4.0 0.0 copy-start.2
  4.0 0.7 copy-done.2
  4.6 0.0 copy-start.3
  4.6 0.7 copy-done.3
  5.3 0.0 copy-start.4
  5.3 0.7 copy-done.4
  5.9 0.0 copy-start.5
  5.9 0.7 copy-done.5
  6.6 0.0 copy-start.6
  6.6 0.7 copy-done.6
  7.2 0.0 copy-start.7
  7.2 0.7 copy-done.7
  7.9 0.7 copy-done.8
  8.6 0.7 copy-done.9
  9.2 56.9 %shifted_scores.1 = (f32[128,8192]{1,0:T(8,128)S(1)}, f32[2,8192]{1,0:T(2,128)S(1)}) custom-call(s32[16]{0:T(128)S(1)} %copy-done.2, f32[16]{0:T(128)S(1)} %copy-done.3, s32[75]{0:T(128)S(1)} %copy-done.9, s32[75]{0:T(128)S(1)} %copy-done.8, s32[8]{0:T(128)S(1)} %copy-done.7, f32[49,8192]{1,0:T(8,128)S(1)} %copy-done, f32[16,49]{1,0:T(8,128)S(1)} %copy-done.1, ...), custom_call_target="tpu_custom_call" | custom-call | tf_op jit(solution)/shard_map/shifted_scores/pallas_call | solution.py:500
  66.1 2.0 %all-gather.1.peaks_ref = f32[2,2,8192]{2,1,0:T(2,128)S(1)} all-gather(f32[1,2,8192]{2,1,0:T(2,128)S(1)} %bitcast.8), channel_id=2, replica_groups=mesh['pairs'=16,'comp'=2] {'comp'}, dimensions={0}, use_global_device_ids=true | all-gather | bytes 196608 | tf_op jit(solution)/shard_map/all_gather | solution.py:596
  68.1 3.1 %finish.1 = (f32[128,8192]{1,0:T(8,128)}, f32[1,8192]{1,0:T(1,128)}, f32[16,128]{1,0:T(8,128)S(1)}) custom-call(f32[128,8192]{1,0:T(8,128)S(1)} %get-tuple-element.8.shifted_ref, f32[2,8192]{1,0:T(2,128)S(1)} %get-tuple-element.9.own_ref, f32[2,2,8192]{2,1,0:T(2,128)S(1)} %all-gather.1.peaks_ref), custom_call_target="tpu_custom_call" | custom-call | tf_op jit(solution)/shard_map/finish/pallas_call | solution.py:577
  71.3 13.8 %all_to_all.9 = f32[16,1,128]{2,1,0:T(1,128)S(1)} all-to-all(f32[16,1,128]{2,1,0:T(1,128)S(1)} %bitcast.9), channel_id=1, replica_groups=mesh['pairs'=16,'comp'=2] {'pairs'}, dimensions={0} | all-to-all | bytes 16384 | tf_op jit(solution)/shard_map/all_to_all | solution.py:599
  85.1 0.5 multiply_log_fusion
  (3 shorter events, 0.0 us)
Async XLA Ops:
  1.8 1.5 %copy-start = (f32[49,8192]{1,0:T(8,128)S(1)}, f32[49,8192]{1,0:T(8,128)}, u32[]{:S(2)}) copy-start(f32[49,8192]{1,0:T(8,128)} %effects_hbm.1) | copy-start | bytes 4816900
  3.3 0.7 copy-start.1
  4.0 0.7 copy-start.2
  4.6 0.7 copy-start.3
  5.3 0.7 copy-start.4
  5.9 0.7 copy-start.5
  6.6 0.7 copy-start.6
  7.2 0.7 copy-start.7
  7.9 0.7 copy-start.8
  8.6 0.7 copy-start.9

commit v8 on v6

--- a/solution.py
+++ b/solution.py
@@ -250,14 +250,14 @@
         x = jnp.where(j < HEAD, x, 0.0)
         for d in range(LANES // SPAN):
             products[pl.ds(d * SPAN, SPAN), :] = x * doubled[pl.ds(d, SPAN), :]
-        for piece, part in enumerate(split3(jnp.transpose(products[...]))):
+        for piece, part in enumerate(split3(jnp.transpose(products[...]))[:2]):
             features[:, piece * LANES : (piece + 1) * LANES] = part
 
     def head_norm():
-        f = [features[:, p * LANES : (p + 1) * LANES] for p in range(3)]
-        w = [form_weights[pl.ds(p * LANES, LANES), :] for p in range(3)]
-        left = jnp.concatenate([f[0], f[0], f[1], f[1], f[0], f[2]], axis=1)
-        right = jnp.concatenate([w[0], w[1], w[0], w[1], w[2], w[0]], axis=0)
+        f = [features[:, p * LANES : (p + 1) * LANES] for p in range(2)]
+        w = [form_weights[pl.ds(p * LANES, LANES), :] for p in range(2)]
+        left = jnp.concatenate([f[0], f[0], f[1], f[1]], axis=1)
+        right = jnp.concatenate([w[0], w[1], w[0], w[1]], axis=0)
         return jnp.dot(left, right, preferred_element_type=jnp.float32)
 
     def prepare(t, target):
@@ -374,7 +374,7 @@
 
         def one_slot(slot, c):
             s = slot - base
-            for piece, part in enumerate(split3(forms[pl.ds(s, LANES, stride=SUB), :])):
+            for piece, part in enumerate(split3(forms[pl.ds(s, LANES, stride=SUB), :])[:2]):
                 form_weights[pl.ds(piece * LANES, LANES), :] = part
             for i in range(HEAD, n):
                 groups = min(i // 16 + 1, even // 16)
@@ -512,10 +512,10 @@
             pltpu.VMEM((SUB, n), f32),
             pltpu.VMEM((HEAD * HEAD * SUB, LANES), f32),
             pltpu.VMEM((LANES * SUB, LANES), f32),
-            pltpu.VMEM((3 * LANES, LANES), jnp.bfloat16),
+            pltpu.VMEM((2 * LANES, LANES), jnp.bfloat16),
             pltpu.VMEM((2 * SPAN, TILE), f32),
             pltpu.VMEM((LANES, TILE), f32),
-            pltpu.VMEM((TILE, 3 * LANES), jnp.bfloat16),
+            pltpu.VMEM((TILE, 2 * LANES), jnp.bfloat16),
             pltpu.SemaphoreType.DMA,
             pltpu.SemaphoreType.DMA,
             pltpu.SemaphoreType.DMA((2,)),

time: 83.1 us -> 81.1 us (0.976)
  Pallas kernels: 60.3 us -> 58.2 us
    pallas_call x1, Pallas kernels: 57.2 us -> 55.1 us  [shifted_scores(): pl.pallas_call(functools.partial(main_kernel, n, tiles, patterns, grid_sc...]
where the time goes in v8:
time: 81.1 us; the launch traced here: 81 us
  Pallas kernels  58.2 us (72%)
  blocking collectives  17 us (21%)
  matrix products  4.15 us (5%)
    pallas_call x1, Pallas kernels, shifted_scores(): pl.pallas_call(functools.partial(main_kernel, n, tiles, patterns, grid_sc...  55.1 us
    all_to_all x1, blocking collectives, per_device(): masses = jnp.sum(lax.all_to_all(mass, 'pairs', 0, 0, tiled=True), axis=0)  15 us
    pallas_call x1, Pallas kernels, finish(): pl.pallas_call(functools.partial(finish_kernel, width), name='finish', in...  3.13 us
    dot_general x1, matrix products, per_device(): jnp.einsum('uij,ukj->uik', base_root, base_root, precision=lax.Precision....  2.33 us
    all_gather x1, blocking collectives, per_device(): peaks = lax.all_gather(peak, 'comp')  2.03 us
    dot_general x1, matrix products, exact_dot(): lax.dot_general(left, right, (dims, ((), ())), precision=lax.Precision.HI...  1.82 us

profile of v8, /device:TPU:0, one launch (start us, length us, event | category | flops | bytes accessed | tf_op | source)
XLA Modules:
  0.0 81.0 jit_solution(1113536259510373452)
XLA Ops:
  0.6 0.0 copy-start.6
  0.6 0.0 copy-start.7
  0.7 0.0 copy-start.8
  0.7 0.0 copy-start.5
  0.7 0.0 copy-start.4
  0.7 0.0 copy-start.3
  0.7 0.0 copy-start.2
  0.7 0.0 copy-start.1
  0.7 0.0 copy-start
  0.7 2.3 %fusion = f32[16,49,49]{2,1,0:T(8,128)S(1)} fusion(f32[16,49,49]{2,0,1:T(8,128)} %param.14), kind=kOutput, calls=%fused_computation | convolution fusion | flops 22588608 | bytes 307328 | tf_op jit(solution)/shard_map/uij,ukj->uik/dot_general | solution.py:586
  3.1 0.2 reshape.12
  3.2 1.8 %fusion.2.covar_hbm = f32[2401,128]{1,0:T(8,128)S(1)} fusion(f32[16,2401]{1,0:T(8,128)S(1)} %reshape.12, s32[128]{0:T(128)} %param.16), kind=kOutput, calls=%fused_computation.3 | convolution fusion | flops 59009024 | bytes 1383488 | tf_op jit(solution)/shard_map/dot_general | solution.py:533
  5.1 0.0 copy-done.6
  5.1 0.0 copy-done.7
  5.1 0.0 copy-done.8
  5.1 0.0 copy-done.5
  5.1 0.0 copy-done.4
  5.1 0.0 copy-done.3
  5.1 0.0 copy-done.2
  5.2 55.1 %shifted_scores.1 = (f32[128,8192]{1,0:T(8,128)S(1)}, f32[2,8192]{1,0:T(2,128)S(1)}) custom-call(s32[16]{0:T(128)S(1)} %copy-done.2, f32[16]{0:T(128)S(1)} %copy-done.3, s32[75]{0:T(128)S(1)} %copy-done.8, s32[75]{0:T(128)S(1)} %copy-done.7, s32[8]{0:T(128)S(1)} %copy-done.6, f32[49,8192]{1,0:T(8,128)S(1)} %copy-done, f32[16,49]{1,0:T(8,128)S(1)} %copy-done.1, ...), custom_call_target="tpu_custom_call" | custom-call | tf_op jit(solution)/shard_map/shifted_scores/pallas_call | solution.py:487
  60.2 2.0 %all-gather.1.peaks_ref = f32[2,2,8192]{2,1,0:T(2,128)S(1)} all-gather(f32[1,2,8192]{2,1,0:T(2,128)S(1)} %bitcast.8), channel_id=2, replica_groups=mesh['pairs'=16,'comp'=2] {'comp'}, dimensions={0}, use_global_device_ids=true | all-gather | bytes 196608 | tf_op jit(solution)/shard_map/all_gather | solution.py:592
  62.3 3.1 %finish.1 = (f32[128,8192]{1,0:T(8,128)}, f32[1,8192]{1,0:T(1,128)}, f32[16,128]{1,0:T(8,128)S(1)}) custom-call(f32[128,8192]{1,0:T(8,128)S(1)} %get-tuple-element.8.shifted_ref, f32[2,8192]{1,0:T(2,128)S(1)} %get-tuple-element.9.own_ref, f32[2,2,8192]{2,1,0:T(2,128)S(1)} %all-gather.1.peaks_ref), custom_call_target="tpu_custom_call" | custom-call | tf_op jit(solution)/shard_map/finish/pallas_call | solution.py:568
  65.4 15.0 %all_to_all.9 = f32[16,1,128]{2,1,0:T(1,128)S(1)} all-to-all(f32[16,1,128]{2,1,0:T(1,128)S(1)} %bitcast.9), channel_id=1, replica_groups=mesh['pairs'=16,'comp'=2] {'pairs'}, dimensions={0} | all-to-all | bytes 16384 | tf_op jit(solution)/shard_map/all_to_all | solution.py:595
  80.4 0.5 multiply_log_fusion
  (3 shorter events, 0.0 us)
Async XLA Ops:
  0.6 4.4 %copy-start.6 = (s32[8]{0:T(128)S(1)}, s32[8]{0:T(128)}, u32[]{:S(2)}) copy-start(s32[8]{0:T(128)} %constant.15.clone.plan_start) | copy-start | bytes 100
  0.6 4.4 %copy-start.7 = (s32[75]{0:T(128)S(1)}, s32[75]{0:T(128)}, u32[]{:S(2)}) copy-start(s32[75]{0:T(128)} %constant.14.clone.plan_col) | copy-start | bytes 904
  0.7 4.4 %copy-start.8 = (s32[75]{0:T(128)S(1)}, s32[75]{0:T(128)}, u32[]{:S(2)}) copy-start(s32[75]{0:T(128)} %constant.13.clone.plan_row) | copy-start | bytes 904
  0.7 4.4 %copy-start.5 = (f32[128]{0:T(128)S(1)}, f32[128]{0:T(128)}, u32[]{:S(2)}) copy-start(f32[128]{0:T(128)} %param.18) | copy-start | bytes 1540
  0.7 4.4 %copy-start.4 = (s32[128]{0:T(128)S(1)}, s32[128]{0:T(128)}, u32[]{:S(2)}) copy-start(s32[128]{0:T(128)} %param.17) | copy-start | bytes 1540
  0.7 4.4 %copy-start.3 = (f32[16]{0:T(128)S(1)}, f32[16]{0:T(128)}, u32[]{:S(2)}) copy-start(f32[16]{0:T(128)} %grid_ref.1) | copy-start | bytes 196
  0.7 4.4 %copy-start.2 = (s32[16]{0:T(128)S(1)}, s32[16]{0:T(128)}, u32[]{:S(2)}) copy-start(s32[16]{0:T(128)} %index_ref.1) | copy-start | bytes 196
  0.7 4.4 %copy-start.1 = (f32[16,49]{1,0:T(8,128)S(1)}, f32[16,49]{1,0:T(8,128)}, u32[]{:S(2)}) copy-start(f32[16,49]{1,0:T(8,128)} %se_ref.1) | copy-start | bytes 9412
  0.7 4.4 %copy-start = (f32[49,8192]{1,0:T(8,128)S(1)}, f32[49,8192]{1,0:T(8,128)}, u32[]{:S(2)}) copy-start(f32[49,8192]{1,0:T(8,128)} %effects_hbm.1) | copy-start | bytes 4816900

commit v9 on v8

--- a/solution.py
+++ b/solution.py
@@ -184,21 +184,30 @@
 
     lax.fori_loop(0, tiles, tally, 0)
 
-    def place(b, state):
-        used, offset = state
-        many = count_s[b]
-        slot_s[used] = b
-        start_s[used] = offset
-        count_s[b] = offset
-        return used + jnp.where(many > 0, 1, 0), offset + many
-
-    used, _ = lax.fori_loop(0, patterns, place, (jnp.int32(0), jnp.int32(0)))
+    def place(least, most):
+        def one(b, state):
+            used, offset = state
+            many = count_s[b]
+            take = jnp.logical_and(many >= least, many <= most)
+
+            @pl.when(take)
+            def _():
+                slot_s[used] = b
+                start_s[used] = offset
+                count_s[b] = offset + tiles + 1
+
+            return used + jnp.where(take, 1, 0), offset + jnp.where(take, many, 0)
+
+        return one
+
+    found = lax.fori_loop(0, patterns, place(2, tiles), (jnp.int32(0), jnp.int32(0)))
+    used, _ = lax.fori_loop(0, patterns, place(1, 1), found)
     start_s[used] = tiles
 
     def sort(t, c):
         b = index_ref[t]
         position = count_s[b]
-        order_s[position] = t
+        order_s[position - tiles - 1] = t
         count_s[b] = position + 1
         return c
 

time: 81.1 us -> 80.7 us (level); the launches traced: 81 us -> 81.4 us
  no operation moved by 1% of the time
where the time goes in v9:
time: 80.7 us; the launch traced here: 81.4 us
  Pallas kernels  58.3 us (72%)
  blocking collectives  17.3 us (21%)
  matrix products  4.15 us (5%)
  between operations  0.81 us (1%)
    pallas_call x1, Pallas kernels, shifted_scores(): pl.pallas_call(functools.partial(main_kernel, n, tiles, patterns, grid_sc...  55.2 us
    all_to_all x1, blocking collectives, per_device(): masses = jnp.sum(lax.all_to_all(mass, 'pairs', 0, 0, tiled=True), axis=0)  15.3 us
    pallas_call x1, Pallas kernels, finish(): pl.pallas_call(functools.partial(finish_kernel, width), name='finish', in...  3.13 us
    dot_general x1, matrix products, per_device(): jnp.einsum('uij,ukj->uik', base_root, base_root, precision=lax.Precision....  2.33 us
    all_gather x1, blocking collectives, per_device(): peaks = lax.all_gather(peak, 'comp')  2.05 us
    dot_general x1, matrix products, exact_dot(): lax.dot_general(left, right, (dims, ((), ())), precision=lax.Precision.HI...  1.82 us

profile of v9, /device:TPU:0, one launch (start us, length us, event | category | flops | bytes accessed | tf_op | source)
XLA Modules:
  0.0 81.4 jit_solution(15176386756676552094)
XLA Ops:
  0.6 0.0 copy-start.6
  0.6 0.0 copy-start.7
  0.7 0.0 copy-start.8
  0.7 0.0 copy-start.5
  0.7 0.0 copy-start.4
  0.7 0.0 copy-start.3
  0.7 0.0 copy-start.2
  0.7 0.0 copy-start.1
  0.7 0.0 copy-start
  0.7 2.3 %fusion = f32[16,49,49]{2,1,0:T(8,128)S(1)} fusion(f32[16,49,49]{2,0,1:T(8,128)} %param.14), kind=kOutput, calls=%fused_computation | convolution fusion | flops 22588608 | bytes 307328 | tf_op jit(solution)/shard_map/uij,ukj->uik/dot_general | solution.py:595
  3.1 0.2 reshape.12
  3.2 1.8 %fusion.2.covar_hbm = f32[2401,128]{1,0:T(8,128)S(1)} fusion(f32[16,2401]{1,0:T(8,128)S(1)} %reshape.12, s32[128]{0:T(128)} %param.16), kind=kOutput, calls=%fused_computation.3 | convolution fusion | flops 59009024 | bytes 1383488 | tf_op jit(solution)/shard_map/dot_general | solution.py:542
  5.1 0.0 copy-done.6
  5.1 0.0 copy-done.7
  5.1 0.0 copy-done.8
  5.1 0.0 copy-done.5
  5.1 0.0 copy-done.4
  5.1 0.0 copy-done.3
  5.1 0.0 copy-done.2
  5.2 55.2 %shifted_scores.1 = (f32[128,8192]{1,0:T(8,128)S(1)}, f32[2,8192]{1,0:T(2,128)S(1)}) custom-call(s32[16]{0:T(128)S(1)} %copy-done.2, f32[16]{0:T(128)S(1)} %copy-done.3, s32[75]{0:T(128)S(1)} %copy-done.8, s32[75]{0:T(128)S(1)} %copy-done.7, s32[8]{0:T(128)S(1)} %copy-done.6, f32[49,8192]{1,0:T(8,128)S(1)} %copy-done, f32[16,49]{1,0:T(8,128)S(1)} %copy-done.1, ...), custom_call_target="tpu_custom_call" | custom-call | tf_op jit(solution)/shard_map/shifted_scores/pallas_call | solution.py:496
  60.4 2.0 %all-gather.1.peaks_ref = f32[2,2,8192]{2,1,0:T(2,128)S(1)} all-gather(f32[1,2,8192]{2,1,0:T(2,128)S(1)} %bitcast.8), channel_id=2, replica_groups=mesh['pairs'=16,'comp'=2] {'comp'}, dimensions={0}, use_global_device_ids=true | all-gather | bytes 196608 | tf_op jit(solution)/shard_map/all_gather | solution.py:601
  62.4 3.1 %finish.1 = (f32[128,8192]{1,0:T(8,128)}, f32[1,8192]{1,0:T(1,128)}, f32[16,128]{1,0:T(8,128)S(1)}) custom-call(f32[128,8192]{1,0:T(8,128)S(1)} %get-tuple-element.8.shifted_ref, f32[2,8192]{1,0:T(2,128)S(1)} %get-tuple-element.9.own_ref, f32[2,2,8192]{2,1,0:T(2,128)S(1)} %all-gather.1.peaks_ref), custom_call_target="tpu_custom_call" | custom-call | tf_op jit(solution)/shard_map/finish/pallas_call | solution.py:577
  65.6 15.3 %all_to_all.9 = f32[16,1,128]{2,1,0:T(1,128)S(1)} all-to-all(f32[16,1,128]{2,1,0:T(1,128)S(1)} %bitcast.9), channel_id=1, replica_groups=mesh['pairs'=16,'comp'=2] {'pairs'}, dimensions={0} | all-to-all | bytes 16384 | tf_op jit(solution)/shard_map/all_to_all | solution.py:604
  80.9 0.5 multiply_log_fusion
  (3 shorter events, 0.0 us)
Async XLA Ops:
  0.6 4.4 %copy-start.6 = (s32[8]{0:T(128)S(1)}, s32[8]{0:T(128)}, u32[]{:S(2)}) copy-start(s32[8]{0:T(128)} %constant.15.clone.plan_start) | copy-start | bytes 100
  0.6 4.4 %copy-start.7 = (s32[75]{0:T(128)S(1)}, s32[75]{0:T(128)}, u32[]{:S(2)}) copy-start(s32[75]{0:T(128)} %constant.14.clone.plan_col) | copy-start | bytes 904
  0.7 4.4 %copy-start.8 = (s32[75]{0:T(128)S(1)}, s32[75]{0:T(128)}, u32[]{:S(2)}) copy-start(s32[75]{0:T(128)} %constant.13.clone.plan_row) | copy-start | bytes 904
  0.7 4.4 %copy-start.5 = (f32[128]{0:T(128)S(1)}, f32[128]{0:T(128)}, u32[]{:S(2)}) copy-start(f32[128]{0:T(128)} %param.18) | copy-start | bytes 1540
  0.7 4.4 %copy-start.4 = (s32[128]{0:T(128)S(1)}, s32[128]{0:T(128)}, u32[]{:S(2)}) copy-start(s32[128]{0:T(128)} %param.17) | copy-start | bytes 1540
  0.7 4.4 %copy-start.3 = (f32[16]{0:T(128)S(1)}, f32[16]{0:T(128)}, u32[]{:S(2)}) copy-start(f32[16]{0:T(128)} %grid_ref.1) | copy-start | bytes 196
  0.7 4.4 %copy-start.2 = (s32[16]{0:T(128)S(1)}, s32[16]{0:T(128)}, u32[]{:S(2)}) copy-start(s32[16]{0:T(128)} %index_ref.1) | copy-start | bytes 196
  0.7 4.4 %copy-start.1 = (f32[16,49]{1,0:T(8,128)S(1)}, f32[16,49]{1,0:T(8,128)}, u32[]{:S(2)}) copy-start(f32[16,49]{1,0:T(8,128)} %se_ref.1) | copy-start | bytes 9412
  0.7 4.4 %copy-start = (f32[49,8192]{1,0:T(8,128)S(1)}, f32[49,8192]{1,0:T(8,128)}, u32[]{:S(2)}) copy-start(f32[49,8192]{1,0:T(8,128)} %effects_hbm.1) | copy-start | bytes 4816900
